TPU v7x, 128 devices: a whole 4x4x4 slice. The times are simulated.
128 devices in a mesh: cols: 32 (over x, z, y_lo), trc: 4 (over y_hi, core).
Axes of the slice: x: 4, y: 4 (y_hi: 2, y_lo: 2; y = y_hi * 2 + y_lo), z: 4, core: 2. Of those that a mesh axis runs over, the one named last changes fastest.
Arguments:
- tracers_src: bfloat16 [28, 127, 65536], P(None, None, ('cols', 'trc')), may hold values from -1 to 2
- layer_dp: float32 [127, 65536], P(None, ('cols', 'trc')), may hold values from 0.3 to 3
- cut_frac: float32 [71, 65536], P(None, ('cols', 'trc')), may hold values from 0.05 to 0.95
- level_bounds: int32 [2, 72, 65536], P(None, None, ('cols', 'trc')), may hold values from 0 to 126, as said below
Outputs:
- remapped_tracers: bfloat16 [28, 72, 65536], P('trc', None, 'cols')
- burden: float32 [28], P('trc')
Inputs may be any that keep to these rules, and one draw needn't show every extreme that they name: level_bounds[0, 0, c] = 0, level_bounds[1, 71, c] = 126, level_bounds[1, t, c] = level_bounds[0, t + 1, c], and level_bounds[0, t, c] rises strictly with t in every column.
All inputs are finite; a program needn't handle non-finite values.
Results may differ from a plain program's by a relative error of at most 0.0005.
Values may be sent and summed in bfloat16 or wider, within the bound.
No kernel may reach another device: no remote copies, remote signals or barrier semaphores. Data moves between devices by JAX's collectives and lax.ppermute only.
A program may use at most 64 MiB of HBM per device.

v0:
```python
import jax
import jax.numpy as jnp
from jax import lax
from jax.sharding import Mesh
from jax.sharding import PartitionSpec as P

TRC = ("trc_0", "trc_1")
COLS = ("cols_0", "cols_1", "cols_2")
COLS_TRC = ("cols_0", "cols_1", "cols_2", "trc_0", "trc_1")


def over_axes(x, axes):
    for axis in axes:
        x = lax.psum(x, axis)
    return x


def remap_block(tracers, layer_dp, cut_frac, bounds):
    columns = layer_dp.shape[1]
    tracer_count = tracers.shape[0]
    layers = layer_dp.shape[0]
    inner_first = bounds[0][1:]
    layer_index = lax.broadcasted_iota(jnp.int32, (1, layers, 1), 1)
    below = (layer_index < inner_first[:, None, :]).astype(jnp.float32)
    inside = (layer_index == inner_first[:, None, :]).astype(jnp.float32)
    intersection = below + cut_frac[:, None, :] * inside
    column_dp = jnp.sum(layer_dp, axis=0, keepdims=True)
    inner_edges = jnp.sum(intersection * layer_dp[None], axis=1)
    targets = jnp.concatenate(
        [jnp.zeros((1, columns), jnp.float32), inner_edges, column_dp], axis=0
    )
    layer_mass = tracers.astype(jnp.float32) * layer_dp[None]
    column_mass = jnp.sum(layer_mass, axis=1)
    inner_mass = jnp.einsum(
        "jsc,qsc->qjc", intersection, layer_mass, precision=lax.Precision.HIGHEST
    )
    edge_mass = jnp.concatenate(
        [jnp.zeros((tracer_count, 1, columns), jnp.float32), inner_mass, column_mass[:, None]],
        axis=1,
    )
    remapped = edge_mass[:, 1:] - edge_mass[:, :-1]
    return (remapped, targets[1:] - targets[:-1], column_mass)


def area_of(first_col, count, total_cols):
    position = first_col + lax.broadcasted_iota(jnp.int32, (count,), 0)
    return 1.0 + 2.0 * position.astype(jnp.float32) / total_cols


def remap_columns(tracers, layer_dp, cut_frac, bounds, start_col, total_cols):
    columns = layer_dp.shape[1]
    block_cols = 128
    tracer_count = tracers.shape[0]
    levels = bounds.shape[1]

    def loop_step(block_index, totals):
        remapped, target_dp, before_part = totals
        offset = block_index * block_cols

        def window(values_in):
            return lax.dynamic_slice_in_dim(values_in, offset, block_cols, values_in.ndim - 1)

        block_mass, block_dp, column_mass = remap_block(
            window(tracers), window(layer_dp), window(cut_frac), window(bounds)
        )
        cell_area = area_of(start_col + offset, block_cols, total_cols)
        before_part = before_part + jnp.sum(column_mass * cell_area[None], axis=1)
        remapped = lax.dynamic_update_slice_in_dim(remapped, block_mass, offset, 2)
        target_dp = lax.dynamic_update_slice_in_dim(target_dp, block_dp, offset, 1)
        return (remapped, target_dp, before_part)

    initial = (
        jnp.zeros((tracer_count, levels, columns), jnp.float32),
        jnp.zeros((levels, columns), jnp.float32),
        jnp.zeros((tracer_count,), jnp.float32),
    )
    return lax.fori_loop(0, columns // block_cols, loop_step, initial)


def burden_terms(remapped, target_dp, start_col, total_cols):
    positive = jnp.maximum(remapped / target_dp[None], 0.0)
    cell_area = area_of(start_col, target_dp.shape[1], total_cols)
    after_part = jnp.sum(positive * target_dp[None] * cell_area[None, None], axis=(1, 2))
    return (positive, after_part)


def per_device(tracers_src, layer_dp, cut_frac, level_bounds):
    groups = lax.axis_size(TRC)
    col_dev = layer_dp.shape[1]
    total_cols = col_dev * lax.axis_size(COLS) * groups
    norm_scale = 1.0 / (total_cols * layer_dp.shape[0])
    start_col = (lax.axis_index(COLS) * groups + lax.axis_index(TRC)) * col_dev
    remapped, target_dp, before_part = remap_columns(
        tracers_src, layer_dp, cut_frac, level_bounds, start_col, total_cols
    )
    positive, after_part = burden_terms(remapped, target_dp, start_col, total_cols)
    before_sum, after_sum = (over_axes(before_part, COLS_TRC), over_axes(after_part, COLS_TRC))
    burden_full = before_sum * norm_scale
    fix_ratio = burden_full / (after_sum * norm_scale)
    local_result = (positive * fix_ratio[:, None, None]).astype(jnp.bfloat16)
    result = lax.all_to_all(local_result, TRC, split_axis=0, concat_axis=2, tiled=True)
    per_group = burden_full.shape[0] // groups
    burden = lax.dynamic_slice_in_dim(burden_full, lax.axis_index(TRC) * per_group, per_group)
    return (result, burden)


def solution(mesh):
    split = Mesh(
        mesh.devices.reshape(4, 4, 2, 2, 2), ("cols_0", "cols_1", "cols_2", "trc_0", "trc_1")
    )
    return jax.shard_map(
        per_device,
        mesh=split,
        in_specs=(
            P(None, None, COLS_TRC),
            P(None, COLS_TRC),
            P(None, COLS_TRC),
            P(None, None, COLS_TRC),
        ),
        out_specs=(P(TRC, None, COLS), P(TRC)),
        check_vma=False,
    )
```

profile of v0, /device:TPU:1, one launch (start us, length us, event | category | flops | bytes accessed | tf_op | source)
XLA Modules:
  0.0 209.9 jit_solution(11570957224502287839)
XLA Ops:
  3.7 129.4 %while.20 = (s32[]{:T(128)}, f32[28,72,512]{2,1,0:T(8,128)}, f32[72,512]{1,0:T(8,128)S(1)}, f32[28]{0:T(128)S(1)}, bf16[28,127,512]{2,1,0:T(8,128)(2,1)}, /*inde...) while((s32[]{:T(128)}, f32[28,72,512]{2,1,0:T(8,128)}, ...), condition=%wide.region_5.0_spmd.clone, body=%wide.region_0.0_spmd.clone.sunk | while | flops 404474784 | bytes 13883509 | solution.py:77
  6.6 5.5 %multiply_reduce_fusion.5 = f32[71,128]{0,1:T(8,128)S(1)} fusion(f32[127,128]{0,1:T(8,128)S(1)} %copy.74, f32[71,128]{0,1:T(8,128)S(1)} %copy.76, s32[71,128]{0,1:T(8,128)S(1)} %bitcast.20), kind=kLoop, calls=%fused_computation.clone.1 | loop fusion | flops 8070144 | bytes 174080 | tf_op jit(solution)/shard_map/while/body/eval_jaxpr/reduce_sum | solution.py:28
  16.0 10.8 %fusion.16 = f32[28,71,128]{1,0,2:T(8,128)} fusion(f32[71,128]{0,1:T(8,128)S(1)} %copy.76, s32[71,128]{0,1:T(8,128)S(1)} %bitcast.21, bf16[28,127,128]{1,0,2:T(8,128)(2,1)S(1)} %copy.73, f32[127,128]{0,1:T(8,128)S(1)} %copy.74), kind=kOutput, calls=%fused_computation.11.clone.1 | convolution fusion | flops 394484352 | bytes 2065920 | tf_op jit(solution)/shard_map/while/body/eval_jaxpr/jsc,qsc->qjc/dot_general | solution.py:34
  27.7 4.7 %maximum_subtract_fusion.4 = f32[28,72,128]{1,0,2:T(8,128)} fusion(f32[28,1,128]{1,0,2:T(8,128)S(1)} %copy.75, f32[28,71,128]{1,0,2:T(8,128)} %fusion.16), kind=kLoop, calls=%fused_computation.8.clone.1 | loop fusion | flops 516096 | bytes 2064384 | tf_op jit(solution)/shard_map/while/body/eval_jaxpr/sub | solution.py:41
  32.4 2.5 %copy.78 = f32[28,72,128]{2,1,0:T(8,128)S(1)} copy(f32[28,72,128]{1,0,2:T(8,128)} %maximum_subtract_fusion.4) | data formatting | bytes 2064384 | tf_op jit(solution)/shard_map/while/body/eval_jaxpr/dynamic_update_slice | solution.py:68
  39.0 5.5 %multiply_reduce_fusion.5 = f32[71,128]{0,1:T(8,128)S(1)} fusion(f32[127,128]{0,1:T(8,128)S(1)} %copy.74, f32[71,128]{0,1:T(8,128)S(1)} %copy.76, s32[71,128]{0,1:T(8,128)S(1)} %bitcast.20), kind=kLoop, calls=%fused_computation.clone.1 | loop fusion | flops 8070144 | bytes 174080 | tf_op jit(solution)/shard_map/while/body/eval_jaxpr/reduce_sum | solution.py:28
  48.4 10.8 %fusion.16 = f32[28,71,128]{1,0,2:T(8,128)} fusion(f32[71,128]{0,1:T(8,128)S(1)} %copy.76, s32[71,128]{0,1:T(8,128)S(1)} %bitcast.21, bf16[28,127,128]{1,0,2:T(8,128)(2,1)S(1)} %copy.73, f32[127,128]{0,1:T(8,128)S(1)} %copy.74), kind=kOutput, calls=%fused_computation.11.clone.1 | convolution fusion | flops 394484352 | bytes 2065920 | tf_op jit(solution)/shard_map/while/body/eval_jaxpr/jsc,qsc->qjc/dot_general | solution.py:34
  60.1 4.7 %maximum_subtract_fusion.4 = f32[28,72,128]{1,0,2:T(8,128)} fusion(f32[28,1,128]{1,0,2:T(8,128)S(1)} %copy.75, f32[28,71,128]{1,0,2:T(8,128)} %fusion.16), kind=kLoop, calls=%fused_computation.8.clone.1 | loop fusion | flops 516096 | bytes 2064384 | tf_op jit(solution)/shard_map/while/body/eval_jaxpr/sub | solution.py:41
  71.4 5.5 %multiply_reduce_fusion.5 = f32[71,128]{0,1:T(8,128)S(1)} fusion(f32[127,128]{0,1:T(8,128)S(1)} %copy.74, f32[71,128]{0,1:T(8,128)S(1)} %copy.76, s32[71,128]{0,1:T(8,128)S(1)} %bitcast.20), kind=kLoop, calls=%fused_computation.clone.1 | loop fusion | flops 8070144 | bytes 174080 | tf_op jit(solution)/shard_map/while/body/eval_jaxpr/reduce_sum | solution.py:28
  80.7 10.8 %fusion.16 = f32[28,71,128]{1,0,2:T(8,128)} fusion(f32[71,128]{0,1:T(8,128)S(1)} %copy.76, s32[71,128]{0,1:T(8,128)S(1)} %bitcast.21, bf16[28,127,128]{1,0,2:T(8,128)(2,1)S(1)} %copy.73, f32[127,128]{0,1:T(8,128)S(1)} %copy.74), kind=kOutput, calls=%fused_computation.11.clone.1 | convolution fusion | flops 394484352 | bytes 2065920 | tf_op jit(solution)/shard_map/while/body/eval_jaxpr/jsc,qsc->qjc/dot_general | solution.py:34
  92.4 4.7 %maximum_subtract_fusion.4 = f32[28,72,128]{1,0,2:T(8,128)} fusion(f32[28,1,128]{1,0,2:T(8,128)S(1)} %copy.75, f32[28,71,128]{1,0,2:T(8,128)} %fusion.16), kind=kLoop, calls=%fused_computation.8.clone.1 | loop fusion | flops 516096 | bytes 2064384 | tf_op jit(solution)/shard_map/while/body/eval_jaxpr/sub | solution.py:41
  103.7 5.5 %multiply_reduce_fusion.5 = f32[71,128]{0,1:T(8,128)S(1)} fusion(f32[127,128]{0,1:T(8,128)S(1)} %copy.74, f32[71,128]{0,1:T(8,128)S(1)} %copy.76, s32[71,128]{0,1:T(8,128)S(1)} %bitcast.20), kind=kLoop, calls=%fused_computation.clone.1 | loop fusion | flops 8070144 | bytes 174080 | tf_op jit(solution)/shard_map/while/body/eval_jaxpr/reduce_sum | solution.py:28
  113.1 10.8 %fusion.16 = f32[28,71,128]{1,0,2:T(8,128)} fusion(f32[71,128]{0,1:T(8,128)S(1)} %copy.76, s32[71,128]{0,1:T(8,128)S(1)} %bitcast.21, bf16[28,127,128]{1,0,2:T(8,128)(2,1)S(1)} %copy.73, f32[127,128]{0,1:T(8,128)S(1)} %copy.74), kind=kOutput, calls=%fused_computation.11.clone.1 | convolution fusion | flops 394484352 | bytes 2065920 | tf_op jit(solution)/shard_map/while/body/eval_jaxpr/jsc,qsc->qjc/dot_general | solution.py:34
  124.8 4.7 %maximum_subtract_fusion.4 = f32[28,72,128]{1,0,2:T(8,128)} fusion(f32[28,1,128]{1,0,2:T(8,128)S(1)} %copy.75, f32[28,71,128]{1,0,2:T(8,128)} %fusion.16), kind=kLoop, calls=%fused_computation.8.clone.1 | loop fusion | flops 516096 | bytes 2064384 | tf_op jit(solution)/shard_map/while/body/eval_jaxpr/sub | solution.py:41
  129.5 2.5 %copy.78 = f32[28,72,128]{2,1,0:T(8,128)S(1)} copy(f32[28,72,128]{1,0,2:T(8,128)} %maximum_subtract_fusion.4) | data formatting | bytes 2064384 | tf_op jit(solution)/shard_map/while/body/eval_jaxpr/dynamic_update_slice | solution.py:68
  133.1 3.1 %multiply_reduce_fusion.2 = f32[28]{0:T(128)S(1)} fusion(f32[512]{0:T(512)} %multiply_add_fusion.1, f32[72,512]{1,0:T(8,128)S(1)} %get-tuple-element.225, f32[28,72,512]{2,1,0:T(8,128)} %get-tuple-element.224), kind=kLoop, calls=%fused_computation.26 | loop fusion | flops 5160932 | bytes 4278384 | tf_op jit(solution)/shard_map/reduce_sum | solution.py:83
  136.2 9.3 %all-reduce.3 = (f32[28]{0:T(128)S(1)}, f32[28]{0:T(128)S(1)}) all-reduce(f32[28]{0:T(128)S(1)} %multiply_reduce_fusion.2, f32[28]{0:T(128)S(1)} %get-tuple-element.226), channel_id=1, replica_groups=mesh['cols_0'=4,'cols_1'=4,'cols_2'=2,'trc_0'=2,'trc_1'=2] {'cols_0'}, use_global_device_ids=true, to_apply=%region_12.0 | all-reduce | flops 56 | bytes 448 | tf_op jit(solution)/shard_map/psum | solution.py:14
  145.5 9.7 %all-reduce.2 = (f32[28]{0:T(128)S(1)}, f32[28]{0:T(128)S(1)}) all-reduce(f32[28]{0:T(128)S(1)} %get-tuple-element.322, f32[28]{0:T(128)S(1)} %get-tuple-element.323), channel_id=1, replica_groups=mesh['cols_0'=4,'cols_1'=4,'cols_2'=2,'trc_0'=2,'trc_1'=2] {'cols_1'}, use_global_device_ids=true, to_apply=%region_13.0 | all-reduce | flops 56 | bytes 448 | tf_op jit(solution)/shard_map/psum | solution.py:14
  155.2 4.1 %all-reduce.6 = (f32[28]{0:T(128)S(1)}, f32[28]{0:T(128)S(1)}) all-reduce(f32[28]{0:T(128)S(1)} %get-tuple-element.320, f32[28]{0:T(128)S(1)} %get-tuple-element.321), channel_id=1, replica_groups=mesh['cols_0'=4,'cols_1'=4,'cols_2'=2,'trc_0'=2,'trc_1'=2] {'cols_2'}, use_global_device_ids=true, to_apply=%region_14.0 | all-reduce | flops 56 | bytes 448 | tf_op jit(solution)/shard_map/psum | solution.py:14
  159.3 5.3 %all-reduce.5 = (f32[28]{0:T(128)S(1)}, f32[28]{0:T(128)S(1)}) all-reduce(f32[28]{0:T(128)S(1)} %get-tuple-element.328, f32[28]{0:T(128)S(1)} %get-tuple-element.329), channel_id=1, replica_groups=mesh['cols_0'=4,'cols_1'=4,'cols_2'=2,'trc_0'=2,'trc_1'=2] {'trc_0'}, use_global_device_ids=true, to_apply=%region_15.0 | all-reduce | flops 56 | bytes 448 | tf_op jit(solution)/shard_map/psum | solution.py:14
  164.6 8.8 %all-reduce.4 = (f32[28]{0:T(128)S(1)}, f32[28]{0:T(128)S(1)}) all-reduce(f32[28]{0:T(128)S(1)} %get-tuple-element.326, f32[28]{0:T(128)S(1)} %get-tuple-element.327), channel_id=1, replica_groups=mesh['cols_0'=4,'cols_1'=4,'cols_2'=2,'trc_0'=2,'trc_1'=2] {'trc_1'}, use_global_device_ids=true, to_apply=%region_16.0 | all-reduce | flops 56 | bytes 448 | tf_op jit(solution)/shard_map/psum | solution.py:14
  173.4 4.3 %multiply_convert_fusion = bf16[28,72,512]{2,1,0:T(8,128)(2,1)} fusion(f32[28]{0:T(128)S(1)} %get-tuple-element.333, f32[28,72,512]{2,1,0:T(8,128)} %get-tuple-element.224, f32[72,512]{1,0:T(8,128)S(1)} %get-tuple-element.225), kind=kLoop, calls=%fused_computation.25 | loop fusion | flops 4128768 | bytes 6340720 | tf_op jit(solution)/shard_map/convert_element_type | solution.py:100
  177.7 4.8 %all-to-all-start = ((bf16[28,72,512]{2,1,0:T(8,128)(2,1)}), bf16[28,72,512]{2,1,0:T(8,128)(2,1)S(1)}, u32[]{:S(2)}, u32[]{:S(2)}) async-start(bf16[28,72,512]{2,1,0:T(8,128)(2,1)} %multiply_convert_fusion), calls=%async_computation | async-start | bytes 4128768 | tf_op jit(solution)/shard_map/all_to_all | solution.py:101
  183.1 25.3 %all-to-all-done = bf16[28,72,512]{2,1,0:T(8,128)(2,1)S(1)} async-done(((bf16[28,72,512]{2,1,0:T(8,128)(2,1)}), bf16[28,72,512]{2,1,0:T(8,128)(2,1)S(1)}, u32[]{:S(2)}, u32[]{:S(2)}) %all-to-all-start) | async-done | bytes 2064416 | tf_op jit(solution)/shard_map/all_to_all | solution.py:101
  (97 shorter events, 45.5 us)
Async XLA Ops:
  15.5 0.5 copy-start
  32.4 3.7 %copy-start.1 = (f32[28]{0:T(128)S(1)}, f32[28]{0:T(128)}, u32[]{:S(2)}) copy-start(f32[28]{0:T(128)} %copy-done) | copy-start | bytes 340 | tf_op jit(solution)/shard_map/while
  47.8 0.5 copy-start
  64.8 3.7 %copy-start.1 = (f32[28]{0:T(128)S(1)}, f32[28]{0:T(128)}, u32[]{:S(2)}) copy-start(f32[28]{0:T(128)} %copy-done) | copy-start | bytes 340 | tf_op jit(solution)/shard_map/while
  80.2 0.5 copy-start
  97.1 3.7 %copy-start.1 = (f32[28]{0:T(128)S(1)}, f32[28]{0:T(128)}, u32[]{:S(2)}) copy-start(f32[28]{0:T(128)} %copy-done) | copy-start | bytes 340 | tf_op jit(solution)/shard_map/while
  112.5 0.5 copy-start
  129.5 3.6 %copy-start.1 = (f32[28]{0:T(128)S(1)}, f32[28]{0:T(128)}, u32[]{:S(2)}) copy-start(f32[28]{0:T(128)} %copy-done) | copy-start | bytes 340 | tf_op jit(solution)/shard_map/while
  177.7 30.7 %all-to-all-start = ((bf16[28,72,512]{2,1,0:T(8,128)(2,1)}), bf16[28,72,512]{2,1,0:T(8,128)(2,1)S(1)}, u32[]{:S(2)}, u32[]{:S(2)}) async-start(bf16[28,72,512]{2,1,0:T(8,128)(2,1)} %multiply_convert_fusion), calls=%async_computation | async-start | bytes 4128768 | tf_op jit(solution)/shard_map/all_to_all | solution.py:101
where the time goes:
time: 211 us; the launch traced here: 210 us
  other arithmetic  55.5 us (26%)
  local copies, waits for them, and re-layouts  43.1 us (20%)
  matrix products  43.1 us (20%)
  blocking collectives  37.2 us (18%)
  waiting for transfers between devices  25.3 us (12%)
  starting transfers between devices  4.81 us (2%)
    dot_general x4, matrix products, remap_block(): jnp.einsum('jsc,qsc->qjc', intersection, layer_mass, precision=lax.Precis...  43.1 us
    psum x5, blocking collectives, over_axes(): x = lax.psum(x, axis)  37.2 us
    all_to_all x1, waiting for transfers between devices, per_device(): lax.all_to_all(local_result, TRC, split_axis=0, concat_axis=2, tiled=True)  25.3 us
    reduce_sum x4, other arithmetic, remap_block(): inner_edges = jnp.sum(intersection * layer_dp[None], axis=1)  21.8 us
    sub x4, other arithmetic, remap_block(): remapped = edge_mass[:, 1:] - edge_mass[:, :-1]  18.9 us
    dynamic_update_slice x8, local copies, waits for them, and re-layouts, loop_step(): remapped = lax.dynamic_update_slice_in_dim(remapped, block_mass, offset, 2)  14.6 us
    dynamic_slice x20, local copies, waits for them, and re-layouts, window(): lax.dynamic_slice_in_dim(values_in, offset, block_cols, values_in.ndim - 1)  13.5 us
    all_to_all x1, starting transfers between devices, per_device(): lax.all_to_all(local_result, TRC, split_axis=0, concat_axis=2, tiled=True)  4.81 us
  transfers between devices with their start and end apart: 1, of which 1 were waited for; matrix products, arithmetic and copies ran while one was open for 0% of the time, Pallas kernels for 0%

commit v1 on v0

v1 whole, which is shorter than its diff:
```python
import functools
import jax, jax.numpy as jnp
from jax import lax
from jax.experimental import pallas as pl
from jax.experimental.pallas import tpu as pltpu
from jax.sharding import Mesh
from jax.sharding import PartitionSpec as P

TRC = ("trc_0", "trc_1")
COLS = ("cols_0", "cols_1", "cols_2")
COLS_TRC = ("cols_0", "cols_1", "cols_2", "trc_0", "trc_1")
F32=jnp.float32; BF=jnp.bfloat16; I32=jnp.int32

def gath(x, idx):
    return jnp.take_along_axis(x, idx, axis=0, mode="promise_in_bounds")

def remap_kernel(meta_ref, tr_ref, dp_ref, cf_ref, lb_ref, o0, o1, o2, o3, s0, s1, s2, s3, part_ref,
                 tri, idx_s, over_s, hi_s, psi_s, inv_s, dbuf, fbuf, *, total_cols, cb0):
    r = pl.program_id(1)
    g = meta_ref[0]
    row8 = lax.broadcasted_iota(I32, (8, 128), 0)
    KT, NV = 72, 9

    def compact(gv, e_masks):
        y = []
        for v in range(15):
            ix = idx_s[8*v:8*v+8, :]
            ov = over_s[8*v:8*v+8, :] != 0
            y.append(jnp.where(ov, gath(gv[v+1], ix), gath(gv[v], ix)))
        out = []
        for o in range(NV):
            m0, m1, m2 = (e_masks[k][8*o:8*o+8, :] != 0 for k in range(3))
            a0 = jnp.where(m0, y[o+1], y[o]); a1 = jnp.where(m0, y[o+3], y[o+2])
            a2 = jnp.where(m0, y[o+5], y[o+4]); a3 = y[o+6]
            c0 = jnp.where(m1, a1, a0); c1 = jnp.where(m1, a3, a2)
            out.append(jnp.where(m2, c1, c0))
        return out

    def diffs(e, total):
        rolled = [pltpu.roll(x, 7, 0) for x in e]
        tb = jnp.broadcast_to(total, (8, 128))
        out = []
        for o in range(NV):
            nxt = rolled[o+1] if o + 1 < NV else tb
            out.append(jnp.where(row8 == 7, nxt, rolled[o]) - e[o])
        return out

    def cums(mass):
        hi = mass.astype(BF)
        mid = (mass - hi.astype(F32)).astype(BF)
        x = jnp.concatenate([hi, mid], axis=0)
        return jnp.dot(tri[...], x, preferred_element_type=F32)

    @pl.when(r == 0)
    def _():
        rr = lax.broadcasted_iota(I32, (128, 256), 0)
        cc = lax.broadcasted_iota(I32, (128, 256), 1) & 127
        tri[...] = (cc < rr).astype(F32).astype(BF)
        b = lb_ref[0]
        jrow = lax.broadcasted_iota(I32, (KT, 128), 0)
        d = b - jrow
        H = d >> 3
        dl = d & 7
        hi_s[0] = H & 1
        hi_s[1] = H & 2
        hi_s[2] = H & 4
        f = jnp.concatenate([jnp.zeros((1, 128), F32), cf_ref[...]], axis=0)
        dbuf[0:8, :] = jnp.zeros((8, 128), I32)
        fbuf[0:8, :] = jnp.zeros((8, 128), F32)
        for v in range(16):
            dv = jnp.zeros((8, 128), I32); fv = jnp.zeros((8, 128), F32)
            for h in range(7):
                o = v - h
                if 0 <= o < NV:
                    sl = slice(8*o, 8*o+8)
                    m = H[sl] == h
                    dv = jnp.where(m, dl[sl], dv)
                    fv = jnp.where(m, f[sl], fv)
            dbuf[8+8*v:16+8*v, :] = dv
            fbuf[8+8*v:16+8*v, :] = fv
            t = row8 + dv
            idx_s[8*v:8*v+8, :] = t & 7
            over_s[8*v:8*v+8, :] = t >> 3
        phi = jnp.zeros((128, 128), F32)
        for k in range(8):
            phi = phi + jnp.where(dbuf[8-k:136-k, :] == k, fbuf[8-k:136-k, :], 0.0)
        srow = lax.broadcasted_iota(I32, (128, 128), 0)
        dpz = jnp.where(srow < 127, dp_ref[...], 0.0)
        psi = phi * dpz
        psi_s[0] = dpz
        psi_s[1] = psi
        c = cums(dpz)
        gg = c + psi
        e = compact([gg[8*v:8*v+8] for v in range(16)], hi_s)
        td = diffs(e, c[127:128])
        for o in range(NV):
            inv_s[8*o:8*o+8, :] = 1.0 / td[o]

    pos_col = meta_ref[1] + (pl.program_id(0) + cb0) * 128 + lax.broadcasted_iota(I32, (1, 128), 1)
    area = 1.0 + 2.0 * pos_col.astype(F32) / total_cols
    last = lax.broadcasted_iota(I32, (128, 128), 0) < 127
    outs = (o0, o1, o2, o3)
    scs = (s0, s1, s2, s3)
    for pair in range(2):
        trs = [jnp.where(last, tr_ref[g ^ (2*pair+i), 0].astype(F32), 0.0) for i in range(2)]
        dpz, psi = psi_s[0], psi_s[1]
        mass = jnp.concatenate([t * dpz for t in trs], axis=1)
        c = cums(mass)
        for i in range(2):
            ci = c[:, 128*i:128*i+128]
            gg = ci + psi * trs[i]
            e = compact([gg[8*v:8*v+8] for v in range(16)], hi_s)
            total = ci[127:128]
            rem = [jnp.maximum(x, 0.0) for x in diffs(e, total)]
            s = rem[0]
            for o in range(1, NV): s = s + rem[o]
            pos = [rem[o] * inv_s[8*o:8*o+8, :] for o in range(NV)]
            mx = pos[0]
            for o in range(1, NV): mx = jnp.maximum(mx, pos[o])
            mx = jnp.max(mx, axis=0, keepdims=True)
            rs = 65535.0 / jnp.maximum(mx, 1e-33)
            code = [((x * rs + 0.5).astype(I32) - 32768) for x in pos]
            outs[2*pair+i][0] = jnp.concatenate(code, axis=0).astype(jnp.int16)
            scs[2*pair+i][0] = mx
            grp = g ^ (2*pair+i)
            part_ref[0, 0, pl.ds(grp, 1), :] = total * area
            part_ref[0, 0, pl.ds(4 + grp, 1), :] = jnp.sum(s, axis=0, keepdims=True) * area

def remap(meta, tr, dp, cf, lb, total_cols, cb0, ncb):
    TRn, KS, C = tr.shape
    KT = lb.shape[1]
    tr4 = tr.reshape(4, TRn // 4, KS, C)
    R = TRn // 4
    col = lambda c, r, m: c + cb0
    gs = pltpu.PrefetchScalarGridSpec(
        num_scalar_prefetch=1, grid=(ncb, R),
        in_specs=[pl.BlockSpec((4, 1, 128, 128), lambda c, r, m: (0, r, 0, c + cb0)),
                  pl.BlockSpec((128, 128), lambda c, r, m: (0, c + cb0)),
                  pl.BlockSpec((KT - 1, 128), lambda c, r, m: (0, c + cb0)),
                  pl.BlockSpec((1, KT, 128), lambda c, r, m: (0, 0, c + cb0))],
        out_specs=[pl.BlockSpec((1, KT, 128), lambda c, r, m: (r, 0, c))] * 4
        + [pl.BlockSpec((1, 1, 128), lambda c, r, m: (r, 0, c))] * 4
        + [pl.BlockSpec((1, 1, 8, 128), lambda c, r, m: (c, r, 0, 0))],
        scratch_shapes=[pltpu.VMEM((128, 256), BF), pltpu.VMEM((128, 128), I32), pltpu.VMEM((128, 128), I32),
                        pltpu.VMEM((3, KT, 128), I32), pltpu.VMEM((2, 128, 128), F32), pltpu.VMEM((KT, 128), F32),
                        pltpu.VMEM((136, 128), I32), pltpu.VMEM((136, 128), F32)])
    return pl.pallas_call(
        functools.partial(remap_kernel, total_cols=total_cols, cb0=cb0),
        grid_spec=gs,
        out_shape=[jax.ShapeDtypeStruct((R, KT, 128 * ncb), jnp.int16)] * 4
        + [jax.ShapeDtypeStruct((R, 1, 128 * ncb), F32)] * 4
        + [jax.ShapeDtypeStruct((ncb, R, 8, 128), F32)],
        name="remap",
    )(meta, tr4, dp, cf, lb)


def finish_kernel(meta_ref, c0, c1, c2, c3, s0, s1, s2, s3, rat_ref, out_ref):
    step = pl.program_id(0)
    for i, (c, s) in enumerate(((c0, s0), (c1, s1), (c2, s2), (c3, s3))):
        @pl.when(step == i)
        def _():
            for r in range(out_ref.shape[0]):
                gain = s[r] * rat_ref[r]
                v = c[r].astype(I32).astype(F32) + 32768.0
                out_ref[r] = (v * gain).astype(BF)


def finish(meta, codes, scales, ratio):
    R, KT, C = codes[0].shape
    full = [pl.BlockSpec(x.shape, lambda s, m: (0, 0, 0)) for x in codes + scales]
    gs = pltpu.PrefetchScalarGridSpec(
        num_scalar_prefetch=1, grid=(4,),
        in_specs=full + [pl.BlockSpec(memory_space=pltpu.SMEM)],
        out_specs=pl.BlockSpec((R, KT, C), lambda s, m: (0, 0, m[0] ^ s)))
    return pl.pallas_call(
        finish_kernel, grid_spec=gs, out_shape=jax.ShapeDtypeStruct((R, KT, 4 * C), BF),
        name="finish")(meta, *codes, *scales, ratio)


def per_device(tracers_src, layer_dp, cut_frac, level_bounds):
    groups = lax.axis_size(TRC)
    col_dev = layer_dp.shape[1]
    total_cols = col_dev * lax.axis_size(COLS) * groups
    norm_scale = 1.0 / (total_cols * layer_dp.shape[0])
    me = lax.axis_index(TRC)
    start_col = (lax.axis_index(COLS) * groups + me) * col_dev
    meta = jnp.stack([me, start_col]).astype(I32)
    res = remap(meta, tracers_src, layer_dp, cut_frac, level_bounds, total_cols, 0, 4)
    codes, scales, part = list(res[:4]), list(res[4:8]), res[8]
    for i in range(1, 4):
        pairs = [(j, j ^ i) for j in range(4)]
        codes[i] = lax.ppermute(codes[i], TRC, pairs)
        scales[i] = lax.ppermute(scales[i], TRC, pairs)
    sums = jnp.sum(part, axis=(0, 3))
    per = sums.shape[0]
    wide = jnp.pad(sums.reshape(1, per * 8), ((0, 0), (0, 128 - per * 8)))
    wide = lax.all_to_all(jnp.broadcast_to(wide, (16, 128)), ("cols_0", "cols_1"), 0, 0, tiled=True).sum(0)
    mine = wide[:per * 8].reshape(per, 2, groups).transpose(2, 1, 0).reshape(1, groups, 2 * per)
    mine = jnp.broadcast_to(mine, (2, groups, 2 * per)).reshape(2 * groups, 2 * per)
    mine = jnp.pad(mine, ((0, 0), (0, 128 - 2 * per)))
    mine = lax.all_to_all(mine, ("cols_2", "trc_0", "trc_1"), 0, 0, tiled=True).sum(0)
    before, after = mine[:per], mine[per:2 * per]
    burden = before * norm_scale
    ratio = burden / (after * norm_scale) / 65535.0
    return (finish(meta, codes, scales, ratio), burden)


def solution(mesh):
    split = Mesh(
        mesh.devices.reshape(4, 4, 2, 2, 2), ("cols_0", "cols_1", "cols_2", "trc_0", "trc_1")
    )
    return jax.shard_map(
        per_device,
        mesh=split,
        in_specs=(
            P(None, None, COLS_TRC),
            P(None, COLS_TRC),
            P(None, COLS_TRC),
            P(None, None, COLS_TRC),
        ),
        out_specs=(P(TRC, None, COLS), P(TRC)),
        check_vma=False,
    )
```

time: 211 us -> 65 us (0.31)
  other arithmetic: 55.5 us -> 2.24 us
  matrix products: 43.1 us -> 0 us
  local copies, waits for them, and re-layouts: 43.1 us -> 2.09 us
  Pallas kernels: 0 us -> 25.3 us
  blocking collectives: 37.2 us -> 13.9 us
  waiting for transfers between devices: 25.3 us -> 4.25 us
  starting transfers between devices: 4.81 us -> 15.7 us
    dot_general x4 -> x0, matrix products: 43.1 us -> none  [remap_block(): jnp.einsum('jsc,qsc->qjc', intersection, layer_mass, precision=lax.Precis...]
    psum x5 -> x0, blocking collectives: 37.2 us -> none  [over_axes(): x = lax.psum(x, axis)]
    reduce_sum x17 -> x3, other arithmetic: 31.3 us -> 1.03 us  [the longest x1 0.99 us: per_device(): sums = jnp.sum(part, axis=(0, 3))]
    pallas_call x0 -> x2, Pallas kernels: none -> 25.3 us  [the longest x1 20.9 us: remap(): pl.pallas_call(functools.partial(remap_kernel, total_cols=total_cols, cb0...]
    all_to_all x1, waiting for transfers between devices: 25.3 us -> 1.58 us  [per_device(): lax.all_to_all(mine, ('cols_2', 'trc_0', 'trc_1'), 0, 0, tiled=True).sum(0)]
    sub x8 -> x0, other arithmetic: 19.3 us -> none  [the longest x4 18.9 us: remap_block(): remapped = edge_mass[:, 1:] - edge_mass[:, :-1]]
    dynamic_update_slice x16 -> x0, local copies, waits for them, and re-layouts: 14.9 us -> none  [the longest x8 14.6 us: loop_step(): remapped = lax.dynamic_update_slice_in_dim(remapped, block_mass, offset, 2)]
    dynamic_slice x21 -> x0, local copies, waits for them, and re-layouts: 14.1 us -> none  [the longest x20 13.5 us: window(): lax.dynamic_slice_in_dim(values_in, offset, block_cols, values_in.ndim - 1)]
  transfers between devices with their start and end apart: 1 -> 7, of which waited for: 1 -> 2; matrix products, arithmetic and copies ran while one was open for 0% -> 4% of each run, Pallas kernels for 0% -> 0%
where the time goes in v1:
time: 65 us; the launch traced here: 64.2 us
  Pallas kernels  25.3 us (39%)
  starting transfers between devices  15.7 us (24%)
  blocking collectives  13.9 us (21%)
  waiting for transfers between devices  4.25 us (7%)
  other arithmetic  2.24 us (3%)
  local copies, waits for them, and re-layouts  2.09 us (3%)
  between operations  0.72 us (1%)
    pallas_call x1, Pallas kernels, remap(): pl.pallas_call(functools.partial(remap_kernel, total_cols=total_cols, cb0...  20.9 us
    all_to_all x1, blocking collectives, per_device(): lax.all_to_all(jnp.broadcast_to(wide, (16, 128)), ('cols_0', 'cols_1'), 0...  13.9 us
    all_to_all x1, starting transfers between devices, per_device(): lax.all_to_all(mine, ('cols_2', 'trc_0', 'trc_1'), 0, 0, tiled=True).sum(0)  6.26 us
    ppermute x3, starting transfers between devices, per_device(): scales[i] = lax.ppermute(scales[i], TRC, pairs)  4.77 us
    ppermute x3, starting transfers between devices, per_device(): codes[i] = lax.ppermute(codes[i], TRC, pairs)  4.69 us
    pallas_call x1, Pallas kernels, finish(): pl.pallas_call(finish_kernel, grid_spec=gs, out_shape=jax.ShapeDtypeStruc...  4.42 us
    ppermute x3, waiting for transfers between devices, per_device(): scales[i] = lax.ppermute(scales[i], TRC, pairs)  2.66 us
    all_to_all x1, waiting for transfers between devices, per_device(): lax.all_to_all(mine, ('cols_2', 'trc_0', 'trc_1'), 0, 0, tiled=True).sum(0)  1.58 us
  transfers between devices with their start and end apart: 7, of which 2 were waited for; matrix products, arithmetic and copies ran while one was open for 4% of the time, Pallas kernels for 0%

profile of v1, /device:TPU:1, one launch (start us, length us, event | category | flops | bytes accessed | tf_op | source)
XLA Modules:
  0.0 64.2 jit_solution(10316176656178949892)
XLA Ops:
  0.6 0.7 %pad_add_fusion.meta_ref = s32[2]{0:T(128)} fusion(s32[1]{0:T(128)} %bitcast.1, s32[1]{0:T(128)} %bitcast), kind=kLoop, calls=%fused_computation | loop fusion | flops 2 | bytes 16 | tf_op jit(solution)/shard_map/stack | solution.py:187
  1.3 20.9 %remap.1 = (s16[7,72,512]{2,1,0:T(8,128)(2,1)}, s16[7,72,512]{2,1,0:T(8,128)(2,1)}, s16[7,72,512]{2,1,0:T(8,128)(2,1)}, s16[7,72,512]{2,1,0:T(8,128)(2,1)}, f32[...) custom-call(s32[2]{0:T(128)} %pad_add_fusion.meta_ref, ...), custom_call_target="tpu_custom_call" | custom-call | tf_op jit(solution)/shard_map/remap/pallas_call | solution.py:147
  22.2 1.5 %collective-permute-start = (s16[7,72,512]{2,1,0:T(8,128)(2,1)}, s16[7,72,512]{2,1,0:T(8,128)(2,1)S(1)}, u32[]{:S(2)}, u32[]{:S(2)}) collective-permute-start(s16[7,72,512]{2,1,0:T(8,128)(2,1)} %get-tuple-element.12), channel_id=1, source_target_pairs={{0,1},{1,0},{2,3},{3,2},{4,5},{5,4},{6,7},{7,6},{8,9},{9,8},{10,11... | collective-permute-start | bytes 1548296 | tf_op jit(solution)/shard_map/ppermute | solution.py:192
  23.6 3.0 %collective-permute-start.1 = (s16[7,72,512]{2,1,0:T(8,128)(2,1)}, s16[7,72,512]{2,1,0:T(8,128)(2,1)S(1)}, u32[]{:S(2)}, u32[]{:S(2)}) collective-permute-start(s16[7,72,512]{2,1,0:T(8,128)(2,1)} %get-tuple-element.13), channel_id=1, source_target_pairs={{0,2},{1,3},{2,0},{3,1},{4,6},{5,7},{6,4},{7,5},{8,10},{9,11},{10,... | collective-permute-start | bytes 1548296 | tf_op jit(solution)/shard_map/ppermute | solution.py:192
  26.7 0.2 collective-permute-start.2
  26.9 0.2 collective-permute-start.3
  27.1 1.0 %reduce_sum.27 = f32[7,8]{1,0:T(8,128)S(1)} reduce(f32[4,7,8,128]{3,2,1,0:T(8,128)} %get-tuple-element.19, f32[]{:T(128)} %constant.32.clone.1), dimensions={0,3}, to_apply=%region_0.0 | reduce | flops 28616 | bytes 114916 | tf_op jit(solution)/shard_map/reduce_sum | solution.py:194
  28.1 0.1 reshape.35
  28.2 13.9 %all_to_all.15 = f32[16,1,128]{2,1,0:T(1,128)S(1)} all-to-all(f32[16,1,128]{2,1,0:T(1,128)S(1)} %broadcast_in_dim.12), channel_id=1, replica_groups=mesh['cols_0'=4,'cols_1'=4,'cols_2'=2,'trc_0'=2,'trc_1'=2] {'cols_0','co..., dimensions={0} | all-to-all | bytes 16384 | tf_op jit(solution)/shard_map/all_to_all | solution.py:197
  42.1 0.1 reshape.36
  42.2 0.1 copy.13
  42.3 0.1 broadcast_in_dim.13
  42.4 0.6 pad.12
  43.0 6.3 %all-to-all-start.1 = ((f32[8,1,128]{2,1,0:T(1,128)}), f32[8,1,128]{2,1,0:T(1,128)S(1)}, u32[]{:S(2)}, u32[]{:S(2)}) async-start(f32[8,1,128]{2,1,0:T(1,128)} %bitcast.8), calls=%async_computation.1 | async-start | bytes 8192 | tf_op jit(solution)/shard_map/all_to_all | solution.py:201
  49.2 2.9 %collective-permute-start.4 = (f32[7,1,512]{2,1,0:T(1,128)}, f32[7,1,512]{2,1,0:T(1,128)S(1)}, u32[]{:S(2)}, u32[]{:S(2)}) collective-permute-start(f32[7,1,512]{2,1,0:T(1,128)} %get-tuple-element.17), channel_id=1, source_target_pairs={{0,2},{1,3},{2,0},{3,1},{4,6},{5,7},{6,4},{7,5},{8,10},{9,11},{10,... | collective-permute-start | bytes 43016 | tf_op jit(solution)/shard_map/ppermute | solution.py:193
  52.1 1.6 %all-to-all-done.1 = f32[8,1,128]{2,1,0:T(1,128)S(1)} async-done(((f32[8,1,128]{2,1,0:T(1,128)}), f32[8,1,128]{2,1,0:T(1,128)S(1)}, u32[]{:S(2)}, u32[]{:S(2)}) %all-to-all-start.1) | async-done | bytes 4128 | tf_op jit(solution)/shard_map/all_to_all | solution.py:201
  53.7 1.7 %collective-permute-start.5 = (f32[7,1,512]{2,1,0:T(1,128)}, f32[7,1,512]{2,1,0:T(1,128)S(1)}, u32[]{:S(2)}, u32[]{:S(2)}) collective-permute-start(f32[7,1,512]{2,1,0:T(1,128)} %get-tuple-element.18), channel_id=1, source_target_pairs={{0,3},{1,2},{2,1},{3,0},{4,7},{5,6},{6,5},{7,4},{8,11},{9,10},{10,... | collective-permute-start | bytes 43016 | tf_op jit(solution)/shard_map/ppermute | solution.py:193
  55.4 0.6 fusion
  56.0 2.7 %collective-permute-done.5.s3 = f32[7,1,512]{2,1,0:T(1,128)S(1)} collective-permute-done((f32[7,1,512]{2,1,0:T(1,128)}, f32[7,1,512]{2,1,0:T(1,128)S(1)}, u32[]{:S(2)}, u32[]{:S(2)}) %collective-permute-start.5) | collective-permute-done | bytes 14368 | tf_op jit(solution)/shard_map/ppermute | solution.py:193
  58.7 0.5 copy-done.5
  59.2 0.2 copy-done
  59.4 0.2 copy-done.1
  59.6 0.1 copy-done.2
  59.8 4.4 %finish.1 = bf16[7,72,2048]{2,1,0:T(8,128)(2,1)} custom-call(s32[2]{0:T(128)} %pad_add_fusion.meta_ref, s16[7,72,512]{2,1,0:T(8,128)(2,1)} %get-tuple-element.11.c0, s16[7,72,512]{2,1,0:T(8,128)(2,1)} %copy-done, s16[7,72,512]{2,1,0:T(8,128)(2,1)} %copy-done.1, s16[7,72,512]{2,1,0:T(8,128)(2,1)} %copy-done.2, f32[7,1,512]{2,1,0:T(1,128)} %get-tuple-element.15.s0, ...), custom_call_target="tpu_custom_call" | custom-call | tf_op jit(solution)/shard_map/finish/pallas_call | solution.py:175
  (18 shorter events, 0.1 us)
Async XLA Ops:
  22.2 36.5 %collective-permute-start = (s16[7,72,512]{2,1,0:T(8,128)(2,1)}, s16[7,72,512]{2,1,0:T(8,128)(2,1)S(1)}, u32[]{:S(2)}, u32[]{:S(2)}) collective-permute-start(s16[7,72,512]{2,1,0:T(8,128)(2,1)} %get-tuple-element.12), channel_id=1, source_target_pairs={{0,1},{1,0},{2,3},{3,2},{4,5},{5,4},{6,7},{7,6},{8,9},{9,8},{10,11... | collective-permute-start | bytes 1548296 | tf_op jit(solution)/shard_map/ppermute | solution.py:192
  23.6 35.0 %collective-permute-start.1 = (s16[7,72,512]{2,1,0:T(8,128)(2,1)}, s16[7,72,512]{2,1,0:T(8,128)(2,1)S(1)}, u32[]{:S(2)}, u32[]{:S(2)}) collective-permute-start(s16[7,72,512]{2,1,0:T(8,128)(2,1)} %get-tuple-element.13), channel_id=1, source_target_pairs={{0,2},{1,3},{2,0},{3,1},{4,6},{5,7},{6,4},{7,5},{8,10},{9,11},{10,... | collective-permute-start | bytes 1548296 | tf_op jit(solution)/shard_map/ppermute | solution.py:192
  26.7 32.0 %collective-permute-start.2 = (s16[7,72,512]{2,1,0:T(8,128)(2,1)}, s16[7,72,512]{2,1,0:T(8,128)(2,1)S(1)}, u32[]{:S(2)}, u32[]{:S(2)}) collective-permute-start(s16[7,72,512]{2,1,0:T(8,128)(2,1)} %get-tuple-element.14), channel_id=1, source_target_pairs={{0,3},{1,2},{2,1},{3,0},{4,7},{5,6},{6,5},{7,4},{8,11},{9,10},{10,... | collective-permute-start | bytes 1548296 | tf_op jit(solution)/shard_map/ppermute | solution.py:192
  26.9 26.8 %collective-permute-start.3 = (f32[7,1,512]{2,1,0:T(1,128)}, f32[7,1,512]{2,1,0:T(1,128)S(1)}, u32[]{:S(2)}, u32[]{:S(2)}) collective-permute-start(f32[7,1,512]{2,1,0:T(1,128)} %get-tuple-element.16), channel_id=1, source_target_pairs={{0,1},{1,0},{2,3},{3,2},{4,5},{5,4},{6,7},{7,6},{8,9},{9,8},{10,11... | collective-permute-start | bytes 43016 | tf_op jit(solution)/shard_map/ppermute | solution.py:193
  43.0 10.7 %all-to-all-start.1 = ((f32[8,1,128]{2,1,0:T(1,128)}), f32[8,1,128]{2,1,0:T(1,128)S(1)}, u32[]{:S(2)}, u32[]{:S(2)}) async-start(f32[8,1,128]{2,1,0:T(1,128)} %bitcast.8), calls=%async_computation.1 | async-start | bytes 8192 | tf_op jit(solution)/shard_map/all_to_all | solution.py:201
  49.2 6.8 %collective-permute-start.4 = (f32[7,1,512]{2,1,0:T(1,128)}, f32[7,1,512]{2,1,0:T(1,128)S(1)}, u32[]{:S(2)}, u32[]{:S(2)}) collective-permute-start(f32[7,1,512]{2,1,0:T(1,128)} %get-tuple-element.17), channel_id=1, source_target_pairs={{0,2},{1,3},{2,0},{3,1},{4,6},{5,7},{6,4},{7,5},{8,10},{9,11},{10,... | collective-permute-start | bytes 43016 | tf_op jit(solution)/shard_map/ppermute | solution.py:193
  53.7 5.0 %copy-start.3 = (f32[7,1,512]{2,1,0:T(1,128)}, f32[7,1,512]{2,1,0:T(1,128)S(1)}, u32[]{:S(2)}) copy-start(f32[7,1,512]{2,1,0:T(1,128)S(1)} %collective-permute-done.3.s1) | copy-start | bytes 43012
  53.7 4.9 %collective-permute-start.5 = (f32[7,1,512]{2,1,0:T(1,128)}, f32[7,1,512]{2,1,0:T(1,128)S(1)}, u32[]{:S(2)}, u32[]{:S(2)}) collective-permute-start(f32[7,1,512]{2,1,0:T(1,128)} %get-tuple-element.18), channel_id=1, source_target_pairs={{0,3},{1,2},{2,1},{3,0},{4,7},{5,6},{6,5},{7,4},{8,11},{9,10},{10,... | collective-permute-start | bytes 43016 | tf_op jit(solution)/shard_map/ppermute | solution.py:193
  56.0 2.7 %copy-start.4 = (f32[7,1,512]{2,1,0:T(1,128)}, f32[7,1,512]{2,1,0:T(1,128)S(1)}, u32[]{:S(2)}) copy-start(f32[7,1,512]{2,1,0:T(1,128)S(1)} %collective-permute-done.4.s2) | copy-start | bytes 43012
  58.6 0.6 copy-start.5
  58.6 0.8 %copy-start = (s16[7,72,512]{2,1,0:T(8,128)(2,1)}, s16[7,72,512]{2,1,0:T(8,128)(2,1)S(1)}, u32[]{:S(2)}) copy-start(s16[7,72,512]{2,1,0:T(8,128)(2,1)S(1)} %collective-permute-done.c1) | copy-start | bytes 1548292
  58.6 1.0 %copy-start.1 = (s16[7,72,512]{2,1,0:T(8,128)(2,1)}, s16[7,72,512]{2,1,0:T(8,128)(2,1)S(1)}, u32[]{:S(2)}) copy-start(s16[7,72,512]{2,1,0:T(8,128)(2,1)S(1)} %collective-permute-done.1.c2) | copy-start | bytes 1548292
  58.7 1.1 %copy-start.2 = (s16[7,72,512]{2,1,0:T(8,128)(2,1)}, s16[7,72,512]{2,1,0:T(8,128)(2,1)S(1)}, u32[]{:S(2)}) copy-start(s16[7,72,512]{2,1,0:T(8,128)(2,1)S(1)} %collective-permute-done.2.c3) | copy-start | bytes 1548292

commit v2 on v0

v2 whole, which is shorter than its diff:
```python
import functools
import jax
import jax.numpy as jnp
from jax import lax
from jax.experimental import pallas as pl
from jax.experimental.pallas import tpu as pltpu
from jax.sharding import Mesh
from jax.sharding import PartitionSpec as P

TRC = ("trc_0", "trc_1")
COLS = ("cols_0", "cols_1", "cols_2")
COLS_TRC = ("cols_0", "cols_1", "cols_2", "trc_0", "trc_1")
F32, BF, I32 = jnp.float32, jnp.bfloat16, jnp.int32
LANES, TILES, OUT = 128, 16, 9

SUBLANE_GATHER = lax.GatherDimensionNumbers(
    offset_dims=(), collapsed_slice_dims=(0,), start_index_map=(0,),
    operand_batching_dims=(1,), start_indices_batching_dims=(1,))


def pick(x, index):
    return lax.gather(x, index[..., None], SUBLANE_GATHER, slice_sizes=(1, 1),
                      mode=lax.GatherScatterMode.PROMISE_IN_BOUNDS)


def tile(x, v):
    return x[8 * v:8 * v + 8]


LEVELS, EXTRA = 72, 8
CHUNKS = (5, 2)


def remap_kernel(first, size, total_cols, tr_ref, *refs):
    if first == 0:
        dp_ref, cf_ref, lb_ref, o0, o1, o2, o3, sum_ref, idx_s, over_s, bit_s, dp_s, psi_s, inv_s, dbuf, fbuf = refs[:16]
        tri, part_s, top_s, fin_s = refs[16:]
    else:
        sum_in, idx_s, over_s, bit_s, dp_s, psi_s, inv_s, o0, o1, o2, o3, sum_ref, tri, part_s, top_s, fin_s = refs
    r = pl.program_id(0)
    groups = lax.axis_size(TRC)
    me = lax.axis_index(TRC)
    cols = tr_ref.shape[3]
    start = (lax.axis_index(COLS) * groups + me) * cols
    row8 = lax.broadcasted_iota(I32, (8, LANES), 0)

    def cums(mass):
        hi = mass.astype(BF)
        mid = (mass - hi.astype(F32)).astype(BF)
        return jnp.dot(tri[...], jnp.concatenate([hi, mid], axis=0), preferred_element_type=F32)

    def edge_differences(cum, extra, cb):
        n = len(cum)
        point = [tile(cum[i], 0) + tile(extra[i], 0) for i in range(n)]
        low = [[None] * 15 for _ in range(n)]
        edge = [[None] * OUT for _ in range(n)]
        roll = [[None] * (OUT + 1) for _ in range(n)]
        diff = [[None] * OUT for _ in range(n)]
        for v in range(15):
            ix = idx_s[cb, 8 * v:8 * v + 8, :]
            ov = over_s[cb, 8 * v:8 * v + 8, :] != 0
            for i in range(n):
                nxt = tile(cum[i], v + 1) + tile(extra[i], v + 1)
                low[i][v] = jnp.where(ov, pick(nxt, ix), pick(point[i], ix))
                point[i] = nxt
            o = v - 6
            if o >= 0:
                m0, m1, m2 = (bit_s[cb, k, 8 * o:8 * o + 8, :] != 0 for k in range(3))
                for i in range(n):
                    y = low[i]
                    a0 = jnp.where(m0, y[o + 1], y[o])
                    a1 = jnp.where(m0, y[o + 3], y[o + 2])
                    a2 = jnp.where(m0, y[o + 5], y[o + 4])
                    c0 = jnp.where(m1, a1, a0)
                    c1 = jnp.where(m1, y[o + 6], a2)
                    edge[i][o] = jnp.where(m2, c1, c0)
                    roll[i][o] = pltpu.roll(edge[i][o], 7, 0)
                    if o > 0:
                        diff[i][o - 1] = jnp.where(row8 == 7, roll[i][o], roll[i][o - 1]) - edge[i][o - 1]
        for i in range(n):
            total = jnp.broadcast_to(cum[i][127:128], (8, LANES))
            diff[i][OUT - 1] = jnp.where(row8 == 7, total, roll[i][OUT - 1]) - edge[i][OUT - 1]
        return diff

    @pl.when(r == 0)
    def _():
        rr = lax.broadcasted_iota(I32, (LANES, 2 * LANES), 0)
        cc = lax.broadcasted_iota(I32, (LANES, 2 * LANES), 1) & (LANES - 1)
        tri[...] = (cc < rr).astype(F32).astype(BF)
        if first:
            return
        dbuf[0:8, :] = jnp.zeros((8, LANES), I32)
        fbuf[0:8, :] = jnp.zeros((8, LANES), F32)

        def prepare(cb, carry):
            at = pl.ds(pl.multiple_of(cb * LANES, LANES), LANES)
            d = lb_ref[0, :, at] - lax.broadcasted_iota(I32, (8 * OUT, LANES), 0)
            high, lowbits = d >> 3, d & 7
            for k in range(3):
                bit_s[cb, k] = high & (1 << k)
            f = jnp.concatenate([jnp.zeros((1, LANES), F32), cf_ref[:, at]], axis=0)
            for v in range(TILES):
                dv, fv = jnp.zeros((8, LANES), I32), jnp.zeros((8, LANES), F32)
                for h in range(7):
                    if 0 <= v - h < OUT:
                        m = tile(high, v - h) == h
                        dv = jnp.where(m, tile(lowbits, v - h), dv)
                        fv = jnp.where(m, tile(f, v - h), fv)
                dbuf[8 + 8 * v:16 + 8 * v, :] = dv
                fbuf[8 + 8 * v:16 + 8 * v, :] = fv
                t = row8 + dv
                idx_s[cb, 8 * v:8 * v + 8, :] = t & 7
                over_s[cb, 8 * v:8 * v + 8, :] = t >> 3
            phi = jnp.zeros((LANES, LANES), F32)
            for k in range(8):
                phi = phi + jnp.where(dbuf[8 - k:136 - k, :] == k, fbuf[8 - k:136 - k, :], 0.0)
            srow = lax.broadcasted_iota(I32, (LANES, LANES), 0)
            dp = jnp.where(srow < 127, dp_ref[:, at], 0.0)
            psi = phi * dp
            dp_s[cb] = dp
            psi_s[cb] = psi
            (thick,) = edge_differences([cums(dp)], [psi], cb)
            for o in range(OUT):
                inv_s[cb, 8 * o:8 * o + 8, :] = 1.0 / thick[o]
            return carry

        lax.fori_loop(0, cols // LANES, prepare, 0, unroll=4)

    outs = (o0, o1, o2, o3)
    real = lax.broadcasted_iota(I32, (LANES, LANES), 0) < 127

    def block(cb, carry):
        at = pl.ds(pl.multiple_of(cb * LANES, LANES), LANES)
        position = start + cb * LANES + lax.broadcasted_iota(I32, (1, LANES), 1)
        area = 1.0 + 2.0 * position.astype(F32) / total_cols
        dp, psi = dp_s[cb], psi_s[cb]
        befores, afters = [], []
        for pair in range(2):
            tr = [jnp.where(real, tr_ref[me ^ (2 * pair + i), 0, :, at].astype(F32), 0.0) for i in range(2)]
            both = cums(jnp.concatenate([t * dp for t in tr], axis=1))
            cum = [both[:, :LANES], both[:, LANES:]]
            diff = edge_differences(cum, [psi * t for t in tr], cb)
            for i in range(2):
                kept = [jnp.maximum(x, 0.0) for x in diff[i]]
                mass = kept[0]
                for o in range(1, OUT):
                    mass = mass + kept[o]
                mean = [kept[o] * inv_s[cb, 8 * o:8 * o + 8, :] for o in range(OUT)]
                top = mean[0]
                for o in range(1, OUT):
                    top = jnp.maximum(top, mean[o])
                top = jnp.max(top, axis=0, keepdims=True)
                step = jnp.ceil(jnp.log2(jnp.maximum(top, 1e-33)) * 256.0)
                scale = 65534.0 / jnp.exp2(step * (1.0 / 256.0))
                code = [(x * scale + 0.5).astype(I32) - 32768 for x in mean]
                rows = pl.ds(pl.multiple_of(r * LEVELS, 8), LEVELS)
                outs[2 * pair + i][rows, at] = jnp.concatenate(code, axis=0).astype(jnp.int16)
                top_s[2 * pair + i, cb, pl.ds(r, 1), :] = step
                befores.append(cum[i][127:128] * area)
                afters.append(jnp.sum(mass, axis=0, keepdims=True) * area)
        return carry + jnp.concatenate(befores + afters, axis=0)

    part_s[r] = lax.fori_loop(0, cols // LANES, block, jnp.zeros((8, LANES), F32), unroll=4)

    @pl.when(r == size - 1)
    def _():
        for i in range(4):
            tops = jnp.concatenate([top_s[i, c] for c in range(cols // LANES)], axis=1)
            outs[i][size * LEVELS:size * LEVELS + EXTRA, :] = tops.astype(I32).astype(jnp.int16)
        lane = lax.broadcasted_iota(I32, (8, LANES), 1)
        acc = jnp.zeros((8, LANES), F32) if first == 0 else sum_in[...]
        for k in range(size):
            acc = jnp.where(lane == first + k, jnp.sum(part_s[k], axis=1, keepdims=True), acc)
        if first == 0:
            sum_ref[...] = acc
        else:
            fin_s[...] = acc
            rows = jnp.concatenate([fin_s[pl.ds(me ^ t, 1), :] for t in range(4)], axis=0)
            late = jnp.concatenate([fin_s[pl.ds(4 + (me ^ t), 1), :] for t in range(4)], axis=0)
            both = jnp.where(lane[:4] < 64, rows, pltpu.roll(late, 64, 1))
            for k in range(sum_ref.shape[0]):
                sum_ref[k] = both


def remap(first, size, tr, dp, cf, lb, shared, sums, total_cols, copies):
    _, _, cols = tr.shape[1:]
    nb = cols // LANES
    whole = pl.BlockSpec(memory_space=pltpu.VMEM)
    ins = [pl.BlockSpec((4, 1, LANES, cols), lambda r: (0, r + first, 0, 0))]
    outs = [pltpu.VMEM((size * LEVELS + EXTRA, cols), jnp.int16)] * 4
    if first == 0:
        args = (tr, dp, cf, lb)
        ins += [
            pl.BlockSpec((LANES, cols), lambda r: (0, 0)),
            pl.BlockSpec((LEVELS - 1, cols), lambda r: (0, 0)),
            pl.BlockSpec((1, LEVELS, cols), lambda r: (0, 0, 0)),
        ]
        outs += [
            pltpu.VMEM((8, LANES), F32),
            pltpu.VMEM((nb, LANES, LANES), I32),
            pltpu.VMEM((nb, LANES, LANES), I32),
            pltpu.VMEM((nb, 3, LEVELS, LANES), I32),
            pltpu.VMEM((nb, LANES, LANES), F32),
            pltpu.VMEM((nb, LANES, LANES), F32),
            pltpu.VMEM((nb, LEVELS, LANES), F32),
        ]
    else:
        args = (tr, sums, *shared)
        ins += [whole] * 7
        outs += [pltpu.VMEM((copies, 4, LANES), F32)]
    scratch = [pltpu.VMEM((136, LANES), I32), pltpu.VMEM((136, LANES), F32)] if first == 0 else []
    return pl.pallas_call(
        functools.partial(remap_kernel, first, size, total_cols),
        grid=(size,), in_specs=ins, out_specs=[whole] * len(outs), out_shape=outs,
        scratch_shapes=scratch + [
            pltpu.VMEM((LANES, 2 * LANES), BF),
            pltpu.VMEM((size, 8, LANES), F32),
            pltpu.VMEM((4, nb, 8, LANES), F32),
            pltpu.VMEM((8, LANES), F32),
        ],
        cost_estimate=pl.CostEstimate(flops=size * 2_000_000_000, bytes_accessed=size * 1_000_000, transcendentals=0),
        compiler_params=pltpu.CompilerParams(vmem_limit_bytes=16 * 2**20),
        name="remap",
    )(*args)


def finish_kernel(meta_ref, *refs, norm):
    n = len(CHUNKS)
    codes, all_ref, out_ref, burden_ref, gain_s = refs[:4 * n], *refs[4 * n:]
    step = pl.program_id(0)

    @pl.when(step == 0)
    def _():
        burden = jnp.sum(all_ref[...], axis=0, keepdims=True) * norm
        burden_ref[...] = burden
        ratio = burden / pltpu.roll(burden, 64, 1)
        gain_s[...] = jnp.broadcast_to(ratio * (1.0 / 65534.0), gain_s.shape)

    for i in range(4):
        @pl.when(step == i)
        def _():
            at = 0
            for c, size in enumerate(CHUNKS):
                ref = codes[i * n + c]
                tops = jnp.exp2(ref[size * LEVELS:size * LEVELS + EXTRA, :].astype(F32) * (1.0 / 256.0))
                for k in range(size):
                    gain = tops[k:k + 1] * gain_s[0:1, at + k:at + k + 1]
                    code = ref[k * LEVELS:(k + 1) * LEVELS, :].astype(F32)
                    out_ref[at + k] = ((code + 32768.0) * gain).astype(BF)
                at += size


def finish(meta, codes, everyone, norm):
    per, cols = sum(CHUNKS), codes[0].shape[1]
    vmem = pl.BlockSpec(memory_space=pltpu.VMEM)
    return pl.pallas_call(
        functools.partial(finish_kernel, norm=norm),
        grid_spec=pltpu.PrefetchScalarGridSpec(
            num_scalar_prefetch=1, grid=(4,), in_specs=[vmem] * (len(codes) + 1),
            out_specs=[pl.BlockSpec((per, LEVELS, cols), lambda s, m: (0, 0, m[0] ^ s)),
                       pl.BlockSpec((1, LANES), lambda s, m: (0, 0))],
            scratch_shapes=[pltpu.VMEM((8, LANES), F32)]),
        out_shape=[jax.ShapeDtypeStruct((per, LEVELS, 4 * cols), BF),
                   jax.ShapeDtypeStruct((1, LANES), F32)],
        compiler_params=pltpu.CompilerParams(vmem_limit_bytes=16 * 2**20),
        name="finish",
    )(meta, *codes, everyone)


def in_vmem(x):
    return pltpu.with_memory_space_constraint(x, pltpu.VMEM)


def in_hbm(x):
    return pltpu.with_memory_space_constraint(x, pltpu.HBM)


def per_device(tracers_src, layer_dp, cut_frac, level_bounds):
    total_cols = layer_dp.shape[1] * lax.axis_size(COLS_TRC)
    norm = 1.0 / (total_cols * layer_dp.shape[0])
    per = tracers_src.shape[0] // 4
    copies = lax.axis_size(COLS)
    tr = in_hbm(tracers_src.reshape(4, per, *tracers_src.shape[1:]))
    layer_dp, cut_frac, level_bounds = in_hbm(layer_dp), in_hbm(cut_frac), in_hbm(level_bounds)
    codes = [[] for _ in range(4)]
    shared = sums = None
    first = 0
    for size in CHUNKS:
        res = remap(first, size, tr, layer_dp, cut_frac, level_bounds, shared, sums, total_cols, copies)
        sums = res[4]
        if first == 0:
            shared = res[5:]
        codes[0].append(res[0])
        for i in range(1, 4):
            moved = lax.ppermute(res[i], TRC, [(j, j ^ i) for j in range(4)])
            codes[i].append(in_vmem(moved))
        first += size
    everyone = lax.all_to_all(sums.reshape(4 * copies, 1, LANES), COLS_TRC, 0, 0, tiled=True)
    everyone = in_vmem(everyone.reshape(4 * copies, LANES))
    meta = lax.axis_index(TRC).astype(I32).reshape(1)
    result, burden = finish(meta, sum(codes, []), everyone, norm)
    return (result, burden[0, :per])


def solution(mesh):
    split = Mesh(
        mesh.devices.reshape(4, 4, 2, 2, 2), ("cols_0", "cols_1", "cols_2", "trc_0", "trc_1")
    )
    return jax.shard_map(
        per_device,
        mesh=split,
        in_specs=(
            P(None, None, COLS_TRC),
            P(None, COLS_TRC),
            P(None, COLS_TRC),
            P(None, None, COLS_TRC),
        ),
        out_specs=(P(TRC, None, COLS), P(TRC)),
        check_vma=False,
    )
```

time: 211 us -> 43.9 us (0.21)
  other arithmetic: 55.5 us -> 0 us
  matrix products: 43.1 us -> 0 us
  local copies, waits for them, and re-layouts: 43.1 us -> 0.51 us
  blocking collectives: 37.2 us -> 0 us
  waiting for transfers between devices: 25.3 us -> 10.4 us
  starting transfers between devices: 4.81 us -> 18.5 us
  Pallas kernels: 0 us -> 13.5 us
    dot_general x4 -> x0, matrix products: 43.1 us -> none  [remap_block(): jnp.einsum('jsc,qsc->qjc', intersection, layer_mass, precision=lax.Precis...]
    psum x5 -> x0, blocking collectives: 37.2 us -> none  [over_axes(): x = lax.psum(x, axis)]
    reduce_sum x17 -> x0, other arithmetic: 31.3 us -> none  [the longest x4 21.8 us: remap_block(): inner_edges = jnp.sum(intersection * layer_dp[None], axis=1)]
    sub x8 -> x0, other arithmetic: 19.3 us -> none  [the longest x4 18.9 us: remap_block(): remapped = edge_mass[:, 1:] - edge_mass[:, :-1]]
    dynamic_update_slice x16 -> x0, local copies, waits for them, and re-layouts: 14.9 us -> none  [the longest x8 14.6 us: loop_step(): remapped = lax.dynamic_update_slice_in_dim(remapped, block_mass, offset, 2)]
    all_to_all x1, waiting for transfers between devices: 25.3 us -> 10.3 us  [per_device(): lax.all_to_all(sums.reshape(4 * copies, 1, LANES), COLS_TRC, 0, 0, tiled=...]
    dynamic_slice x21 -> x0, local copies, waits for them, and re-layouts: 14.1 us -> none  [the longest x20 13.5 us: window(): lax.dynamic_slice_in_dim(values_in, offset, block_cols, values_in.ndim - 1)]
    pallas_call x0 -> x3, Pallas kernels: none -> 13.5 us  [the longest x2 11.2 us: remap(): pl.pallas_call(functools.partial(remap_kernel, first, size, total_cols),...]
  transfers between devices with their start and end apart: 1 -> 7, of which waited for: 1 -> 1; matrix products, arithmetic and copies ran while one was open for 0% -> 0% of each run, Pallas kernels for 0% -> 9%
where the time goes in v2:
time: 43.9 us; the launch traced here: 43.6 us
  starting transfers between devices  18.5 us (42%)
  Pallas kernels  13.5 us (31%)
  waiting for transfers between devices  10.4 us (24%)
  between operations  0.67 us (2%)
  local copies, waits for them, and re-layouts  0.51 us (1%)
    pallas_call x2, Pallas kernels, remap(): pl.pallas_call(functools.partial(remap_kernel, first, size, total_cols),...  11.2 us
    all_to_all x1, waiting for transfers between devices, per_device(): lax.all_to_all(sums.reshape(4 * copies, 1, LANES), COLS_TRC, 0, 0, tiled=...  10.3 us
    all_to_all x1, starting transfers between devices, per_device(): lax.all_to_all(sums.reshape(4 * copies, 1, LANES), COLS_TRC, 0, 0, tiled=...  9.43 us
    ppermute x6, starting transfers between devices, per_device(): moved = lax.ppermute(res[i], TRC, [(j, j ^ i) for j in range(4)])  9.11 us
    pallas_call x1, Pallas kernels, finish(): pl.pallas_call(functools.partial(finish_kernel, norm=norm), grid_spec=plt...  2.34 us
  transfers between devices with their start and end apart: 7, of which 1 were waited for; matrix products, arithmetic and copies ran while one was open for 0% of the time, Pallas kernels for 9%

profile of v2, /device:TPU:1, one launch (start us, length us, event | category | flops | bytes accessed | tf_op | source)
XLA Modules:
  0.0 43.6 jit_solution(12819433753483364153)
XLA Ops:
  0.6 7.2 %remap.2 = (s16[368,512]{1,0:T(8,128)(2,1)S(1)}, s16[368,512]{1,0:T(8,128)(2,1)S(1)}, s16[368,512]{1,0:T(8,128)(2,1)S(1)}, s16[368,512]{1,0:T(8,128)(2,1)S(1)}, ...) custom-call(bf16[4,7,127,512]{3,2,1,0:T(8,128)(2,1)} %bitcast.9, ...), custom_call_target="tpu_custom_call" | custom-call | flops 10000000000 | bytes 5000000 | tf_op jit(solution)/shard_map/remap/pallas_call | solution.py:212
  7.9 1.4 %collective-permute-start = (s16[368,512]{1,0:T(8,128)(2,1)S(1)}, s16[368,512]{1,0:T(8,128)(2,1)S(1)}, u32[]{:S(2)}, u32[]{:S(2)}) collective-permute-start(s16[368,512]{1,0:T(8,128)(2,1)S(1)} %get-tuple-element.29), channel_id=1, source_target_pairs={{0,1},{1,0},{2,3},{3,2},{4,5},{5,4},{6,7},{7,6},{8,9},{9,8},{10,11... | collective-permute-start | bytes 1130504 | tf_op jit(solution)/shard_map/ppermute | solution.py:295
  9.3 3.0 %collective-permute-start.2 = (s16[368,512]{1,0:T(8,128)(2,1)S(1)}, s16[368,512]{1,0:T(8,128)(2,1)S(1)}, u32[]{:S(2)}, u32[]{:S(2)}) collective-permute-start(s16[368,512]{1,0:T(8,128)(2,1)S(1)} %get-tuple-element.31), channel_id=1, source_target_pairs={{0,2},{1,3},{2,0},{3,1},{4,6},{5,7},{6,4},{7,5},{8,10},{9,11},{10,... | collective-permute-start | bytes 1130504 | tf_op jit(solution)/shard_map/ppermute | solution.py:295
  12.3 0.2 collective-permute-start.4
  12.5 3.9 %remap.3 = (s16[152,512]{1,0:T(8,128)(2,1)S(1)}, s16[152,512]{1,0:T(8,128)(2,1)S(1)}, s16[152,512]{1,0:T(8,128)(2,1)}, s16[152,512]{1,0:T(8,128)(2,1)S(1)}, f32[32,4,128]{2,1,0:T(4,128)}) custom-call(bf16[4,7,127,512]{3,2,1,0:T(8,128)(2,1)} %bitcast.10, f32[8,128]{1,0:T(8,128)S(1)} %get-tuple-element.21.refs_0_, ...), custom_call_target="tpu_custom_call" | custom-call | flops 4000000000 | bytes 2000000 | tf_op jit(solution)/shard_map/remap/pallas_call | solution.py:212
  16.5 0.2 collective-permute-start.1
  16.7 3.0 %collective-permute-start.3 = (s16[152,512]{1,0:T(8,128)(2,1)}, s16[152,512]{1,0:T(8,128)(2,1)S(1)}, u32[]{:S(2)}, u32[]{:S(2)}) collective-permute-start(s16[152,512]{1,0:T(8,128)(2,1)} %get-tuple-element.32), channel_id=1, source_target_pairs={{0,2},{1,3},{2,0},{3,1},{4,6},{5,7},{6,4},{7,5},{8,10},{9,11},{10,... | collective-permute-start | bytes 466952 | tf_op jit(solution)/shard_map/ppermute | solution.py:295
  19.6 0.0 collective-permute-done.1.refs_3_
  19.6 1.3 %collective-permute-start.5 = (s16[152,512]{1,0:T(8,128)(2,1)S(1)}, s16[152,512]{1,0:T(8,128)(2,1)S(1)}, u32[]{:S(2)}, u32[]{:S(2)}) collective-permute-start(s16[152,512]{1,0:T(8,128)(2,1)S(1)} %get-tuple-element.34), channel_id=1, source_target_pairs={{0,3},{1,2},{2,1},{3,0},{4,7},{5,6},{6,5},{7,4},{8,11},{9,10},{10,... | collective-permute-start | bytes 466952 | tf_op jit(solution)/shard_map/ppermute | solution.py:295
  20.9 9.4 %all-to-all-start = ((f32[128,1,128]{2,1,0:T(1,128)}), f32[128,1,128]{2,1,0:T(1,128)S(1)}, u32[]{:S(2)}, u32[]{:S(2)}) async-start(f32[128,1,128]{2,1,0:T(1,128)} %bitcast.3), calls=%async_computation | async-start | bytes 131072 | tf_op jit(solution)/shard_map/all_to_all | solution.py:298
  30.4 10.3 %all-to-all-done = f32[128,1,128]{2,1,0:T(1,128)S(1)} async-done(((f32[128,1,128]{2,1,0:T(1,128)}), f32[128,1,128]{2,1,0:T(1,128)S(1)}, u32[]{:S(2)}, u32[]{:S(2)}) %all-to-all-start) | async-done | bytes 65568 | tf_op jit(solution)/shard_map/all_to_all | solution.py:298
  40.7 0.0 collective-permute-done.3.refs_5_
  40.7 0.0 collective-permute-done.5.refs_7_
  40.7 0.0 collective-permute-done.refs_2_
  40.7 0.0 collective-permute-done.2.refs_4_
  40.7 0.0 collective-permute-done.4.refs_6_
  40.7 2.3 %finish.1 = (bf16[7,72,2048]{2,1,0:T(8,128)(2,1)}, f32[1,128]{1,0:T(1,128)S(1)}) custom-call(s32[1]{0:T(128)} %bitcast.meta_ref, s16[368,512]{1,0:T(8,128)(2,1)S(1)} %get-tuple-element.20.refs_0_, s16[152,512]{1,0:T(8,128)(2,1)S(1)} %get-tuple-element.28.refs_1_, s16[368,512]{1,0:T(8,128)(2,1)S(1)} %collective-permute-done.refs_2_, ...), custom_call_target="tpu_custom_call" | custom-call | tf_op jit(solution)/shard_map/finish/pallas_call | solution.py:256
  43.1 0.5 %slice_bitcast_fusion = f32[7]{0:T(128)} fusion(f32[1,128]{1,0:T(1,128)S(1)} %get-tuple-element.37), kind=kLoop, calls=%fused_computation | loop fusion | bytes 56 | tf_op jit(solution)/shard_map/squeeze | solution.py:302
Async XLA Ops:
  7.9 32.8 %collective-permute-start = (s16[368,512]{1,0:T(8,128)(2,1)S(1)}, s16[368,512]{1,0:T(8,128)(2,1)S(1)}, u32[]{:S(2)}, u32[]{:S(2)}) collective-permute-start(s16[368,512]{1,0:T(8,128)(2,1)S(1)} %get-tuple-element.29), channel_id=1, source_target_pairs={{0,1},{1,0},{2,3},{3,2},{4,5},{5,4},{6,7},{7,6},{8,9},{9,8},{10,11... | collective-permute-start | bytes 1130504 | tf_op jit(solution)/shard_map/ppermute | solution.py:295
  9.3 31.4 %collective-permute-start.2 = (s16[368,512]{1,0:T(8,128)(2,1)S(1)}, s16[368,512]{1,0:T(8,128)(2,1)S(1)}, u32[]{:S(2)}, u32[]{:S(2)}) collective-permute-start(s16[368,512]{1,0:T(8,128)(2,1)S(1)} %get-tuple-element.31), channel_id=1, source_target_pairs={{0,2},{1,3},{2,0},{3,1},{4,6},{5,7},{6,4},{7,5},{8,10},{9,11},{10,... | collective-permute-start | bytes 1130504 | tf_op jit(solution)/shard_map/ppermute | solution.py:295
  12.3 28.4 %collective-permute-start.4 = (s16[368,512]{1,0:T(8,128)(2,1)S(1)}, s16[368,512]{1,0:T(8,128)(2,1)S(1)}, u32[]{:S(2)}, u32[]{:S(2)}) collective-permute-start(s16[368,512]{1,0:T(8,128)(2,1)S(1)} %get-tuple-element.33), channel_id=1, source_target_pairs={{0,3},{1,2},{2,1},{3,0},{4,7},{5,6},{6,5},{7,4},{8,11},{9,10},{10,... | collective-permute-start | bytes 1130504 | tf_op jit(solution)/shard_map/ppermute | solution.py:295
  16.5 3.2 %collective-permute-start.1 = (s16[152,512]{1,0:T(8,128)(2,1)S(1)}, s16[152,512]{1,0:T(8,128)(2,1)S(1)}, u32[]{:S(2)}, u32[]{:S(2)}) collective-permute-start(s16[152,512]{1,0:T(8,128)(2,1)S(1)} %get-tuple-element.30), channel_id=1, source_target_pairs={{0,1},{1,0},{2,3},{3,2},{4,5},{5,4},{6,7},{7,6},{8,9},{9,8},{10,11... | collective-permute-start | bytes 466952 | tf_op jit(solution)/shard_map/ppermute | solution.py:295
  16.7 24.0 %collective-permute-start.3 = (s16[152,512]{1,0:T(8,128)(2,1)}, s16[152,512]{1,0:T(8,128)(2,1)S(1)}, u32[]{:S(2)}, u32[]{:S(2)}) collective-permute-start(s16[152,512]{1,0:T(8,128)(2,1)} %get-tuple-element.32), channel_id=1, source_target_pairs={{0,2},{1,3},{2,0},{3,1},{4,6},{5,7},{6,4},{7,5},{8,10},{9,11},{10,... | collective-permute-start | bytes 466952 | tf_op jit(solution)/shard_map/ppermute | solution.py:295
  19.6 21.1 %collective-permute-start.5 = (s16[152,512]{1,0:T(8,128)(2,1)S(1)}, s16[152,512]{1,0:T(8,128)(2,1)S(1)}, u32[]{:S(2)}, u32[]{:S(2)}) collective-permute-start(s16[152,512]{1,0:T(8,128)(2,1)S(1)} %get-tuple-element.34), channel_id=1, source_target_pairs={{0,3},{1,2},{2,1},{3,0},{4,7},{5,6},{6,5},{7,4},{8,11},{9,10},{10,... | collective-permute-start | bytes 466952 | tf_op jit(solution)/shard_map/ppermute | solution.py:295
  20.9 19.8 %all-to-all-start = ((f32[128,1,128]{2,1,0:T(1,128)}), f32[128,1,128]{2,1,0:T(1,128)S(1)}, u32[]{:S(2)}, u32[]{:S(2)}) async-start(f32[128,1,128]{2,1,0:T(1,128)} %bitcast.3), calls=%async_computation | async-start | bytes 131072 | tf_op jit(solution)/shard_map/all_to_all | solution.py:298

commit v3 on v0

v3 whole, which is shorter than its diff:
```python
import functools
import jax
import jax.numpy as jnp
from jax import lax
from jax.experimental import pallas as pl
from jax.experimental.pallas import tpu as pltpu
from jax.sharding import Mesh
from jax.sharding import PartitionSpec as P

TRC = ("trc_0", "trc_1")
COLS = ("cols_0", "cols_1", "cols_2")
COLS_TRC = ("cols_0", "cols_1", "cols_2", "trc_0", "trc_1")
F32, BF, I32, I16 = jnp.float32, jnp.bfloat16, jnp.int32, jnp.int16
LANES, TILES, OUT = 128, 16, 9
LAYERS, LEVELS, EXTRA = 127, 72, 8
EARLY, LATE = 5, 2

SUBLANE_GATHER = lax.GatherDimensionNumbers(
    offset_dims=(), collapsed_slice_dims=(0,), start_index_map=(0,),
    operand_batching_dims=(1,), start_indices_batching_dims=(1,))


def pick(x, index):
    return lax.gather(x, index[..., None], SUBLANE_GATHER, slice_sizes=(1, 1),
                      mode=lax.GatherScatterMode.PROMISE_IN_BOUNDS)


def tile(x, v):
    return x[8 * v:8 * v + 8]


def row_in_tile():
    return lax.broadcasted_iota(I32, (8, LANES), 0)


def cumulate(tri, mass):
    hi = mass.astype(BF)
    mid = (mass - hi.astype(F32)).astype(BF)
    return jnp.dot(tri[...], jnp.concatenate([hi, mid], axis=0), preferred_element_type=F32)


def edge_differences(cum, extra, cb, idx_s, over_s, one_s, two_s, four_s):
    n = len(cum)
    row8 = row_in_tile()
    y = [[None] * 15 for _ in range(n)]
    z = [[None] * 15 for _ in range(n)]
    w = [[None] * 13 for _ in range(n)]
    edge = [[None] * OUT for _ in range(n)]
    roll = [[None] * OUT for _ in range(n)]
    diff = [[None] * OUT for _ in range(n)]
    point = [tile(cum[i], 0) + extra(i, 0) for i in range(n)]
    for v in range(15):
        ix = idx_s[cb, 8 * v:8 * v + 8, :]
        over = over_s[cb, 8 * v:8 * v + 8, :] != 0
        for i in range(n):
            nxt = tile(cum[i], v + 1) + extra(i, v + 1)
            y[i][v] = jnp.where(over, pick(nxt, ix), pick(point[i], ix))
            point[i] = nxt
        a = v - 1
        if a >= 0:
            m = one_s[cb, 8 * a:8 * a + 8, :] != 0
            for i in range(n):
                z[i][a] = jnp.where(m, y[i][a + 1], y[i][a])
        if v == 14:
            for i in range(n):
                z[i][14] = y[i][14]
        for b in ([v - 3] if v < 14 else [11, 12]):
            if b < 0:
                continue
            m = two_s[cb, 8 * b:8 * b + 8, :] != 0
            for i in range(n):
                w[i][b] = jnp.where(m, z[i][b + 2], z[i][b])
            o = b - 4
            if o < 0:
                continue
            m = four_s[cb, 8 * o:8 * o + 8, :] != 0
            for i in range(n):
                edge[i][o] = jnp.where(m, w[i][o + 4], w[i][o])
                roll[i][o] = pltpu.roll(edge[i][o], 7, 0)
                if o > 0:
                    diff[i][o - 1] = jnp.where(row8 == 7, roll[i][o], roll[i][o - 1]) - edge[i][o - 1]
    for i in range(n):
        total = jnp.broadcast_to(cum[i][LAYERS:LAYERS + 1], (8, LANES))
        diff[i][OUT - 1] = jnp.where(row8 == 7, total, roll[i][OUT - 1]) - edge[i][OUT - 1]
    return diff


def prepare(dp_ref, cf_ref, lb_ref, tri, idx_s, over_s, one_s, two_s, four_s, dp_s, psi_s, inv_s, dbuf, fbuf):
    rr = lax.broadcasted_iota(I32, (LANES, 2 * LANES), 0)
    cc = lax.broadcasted_iota(I32, (LANES, 2 * LANES), 1) & (LANES - 1)
    tri[...] = (cc < rr).astype(F32).astype(BF)
    row8 = row_in_tile()
    zero_i, zero_f = jnp.zeros((8, LANES), I32), jnp.zeros((8, LANES), F32)
    for cb in range(dp_s.shape[0]):
        dbuf[cb, 0:8, :] = zero_i
        fbuf[cb, 0:8, :] = zero_f
        at = slice(cb * LANES, (cb + 1) * LANES)
        d = lb_ref[0, :, at] - lax.broadcasted_iota(I32, (LEVELS, LANES), 0)
        high, low = d >> 3, d & 7
        f = jnp.concatenate([jnp.zeros((1, LANES), F32), cf_ref[:, at]], axis=0)
        for v in range(TILES):
            dv, fv = zero_i, zero_f
            for h in range(7):
                if 0 <= v - h < OUT:
                    m = tile(high, v - h) == h
                    dv = jnp.where(m, tile(low, v - h), dv)
                    fv = jnp.where(m, tile(f, v - h), fv)
            dbuf[cb, 8 + 8 * v:16 + 8 * v, :] = dv
            fbuf[cb, 8 + 8 * v:16 + 8 * v, :] = fv
            t = row8 + dv
            idx_s[cb, 8 * v:8 * v + 8, :] = t & 7
            over_s[cb, 8 * v:8 * v + 8, :] = t >> 3
        for v in range(14):
            bit = zero_i
            for h in (0, 2, 4, 6):
                if 0 <= v - h < OUT:
                    bit = jnp.where(tile(high, v - h) == h + 1, 1, bit)
            one_s[cb, 8 * v:8 * v + 8, :] = bit
        for v in range(13):
            bit = zero_i
            for h in (0, 4):
                if 0 <= v - h < OUT:
                    bit = jnp.where((tile(high, v - h) >> 1) == (h >> 1) + 1, 1, bit)
            two_s[cb, 8 * v:8 * v + 8, :] = bit
        four_s[cb] = high >> 2
        phi = jnp.zeros((LANES, LANES), F32)
        for k in range(8):
            phi = phi + jnp.where(dbuf[cb, 8 - k:136 - k, :] == k, fbuf[cb, 8 - k:136 - k, :], 0.0)
        dp = jnp.concatenate([dp_ref[:, at], jnp.zeros((1, LANES), F32)], axis=0)
        psi = phi * dp
        dp_s[cb] = dp
        psi_s[cb] = psi
        (thick,) = edge_differences(
            [cumulate(tri, dp)], lambda i, v: tile(psi, v), cb, idx_s, over_s, one_s, two_s, four_s)
        for o in range(OUT):
            inv_s[cb, 8 * o:8 * o + 8, :] = 1.0 / thick[o]


def remap_step(r, tr_ref, outs, tabs, extra_s, part_s, top_s, total_cols):
    tri, idx_s, over_s, one_s, two_s, four_s, dp_s, psi_s, inv_s = tabs
    me = lax.axis_index(TRC)
    blocks = dp_s.shape[0]
    start = (lax.axis_index(COLS) * lax.axis_size(TRC) + me) * blocks * LANES
    before, after = [None] * 4, [None] * 4
    for cb in range(blocks):
        at = slice(cb * LANES, (cb + 1) * LANES)
        position = start + cb * LANES + lax.broadcasted_iota(I32, (1, LANES), 1)
        area = 1.0 + 2.0 * position.astype(F32) / total_cols
        for pair in (0, 2):
            mass = []
            for i in range(2):
                t = tr_ref[me ^ (pair + i), :, at].astype(F32)
                t = jnp.concatenate([t, jnp.zeros((1, LANES), F32)], axis=0)
                mass.append(t * dp_s[cb])
                extra_s[cb, pair + i] = t * psi_s[cb]
            both = cumulate(tri, jnp.concatenate(mass, axis=1))
            cum = [both[:, :LANES], both[:, LANES:]]
            diff = edge_differences(
                cum, lambda i, v: extra_s[cb, pair + i, 8 * v:8 * v + 8, :], cb, idx_s, over_s, one_s, two_s, four_s)
            for i in range(2):
                k = pair + i
                kept = [jnp.maximum(x, 0.0) for x in diff[i]]
                mean = [kept[o] * inv_s[cb, 8 * o:8 * o + 8, :] for o in range(OUT)]
                sums, top = kept[0], mean[0]
                for o in range(1, OUT):
                    sums, top = sums + kept[o], jnp.maximum(top, mean[o])
                top = jnp.max(top, axis=0, keepdims=True)
                step = jnp.ceil(jnp.log2(jnp.maximum(top, 1e-33)) * 256.0)
                scale = 65534.0 / jnp.exp2(step * (1.0 / 256.0))
                code = jnp.concatenate([(x * scale + 0.5).astype(I32) for x in mean], axis=0)
                rows = pl.ds(pl.multiple_of(r * LEVELS, 8), LEVELS)
                outs[k][rows, at] = code.astype(I16)
                top_s[k, cb, pl.ds(r, 1), :] = step
                last, area_sum = cum[i][LAYERS:LAYERS + 1] * area, sums * area
                before[k] = last if cb == 0 else before[k] + last
                after[k] = area_sum if cb == 0 else after[k] + area_sum
    part_s[r] = jnp.concatenate(before + [jnp.sum(x, axis=0, keepdims=True) for x in after], axis=0)


def close(first, size, outs, part_s, top_s, acc):
    for i in range(4):
        tops = jnp.concatenate([top_s[i, c] for c in range(top_s.shape[1])], axis=1)
        outs[i][size * LEVELS:size * LEVELS + EXTRA, :] = tops.astype(I32).astype(I16)
    lane = lax.broadcasted_iota(I32, (8, LANES), 1)
    for k in range(size):
        acc = jnp.where(lane == first + k, jnp.sum(part_s[k], axis=1, keepdims=True), acc)
    return acc


def early_kernel(total_cols, tr_hbm, dp_ref, cf_ref, lb_ref, *refs):
    outs, sum_ref, next_ref, tabs = refs[:4], refs[4], refs[5], refs[6:15]
    dbuf, fbuf, held, sems, extra_s, part_s, top_s = refs[15:]
    r = pl.program_id(0)

    def copy(k):
        dst = held.at[k] if k < EARLY else next_ref.at[k - EARLY]
        return pltpu.make_async_copy(tr_hbm.at[:, k], dst, sems.at[k])

    @pl.when(r == 0)
    def _():
        for k in range(EARLY + LATE):
            copy(k).start()
        prepare(dp_ref, cf_ref, lb_ref, *tabs, dbuf, fbuf)

    pltpu.make_async_copy(tr_hbm.at[:, r], held.at[r], sems.at[r]).wait()
    remap_step(r, held.at[r], outs, tabs, extra_s, part_s, top_s, total_cols)

    @pl.when(r == EARLY - 1)
    def _():
        sum_ref[...] = close(0, EARLY, outs, part_s, top_s, jnp.zeros((8, LANES), F32))
        for k in range(EARLY, EARLY + LATE):
            copy(k).wait()


def late_kernel(total_cols, sum_in, tr_ref, *refs):
    tabs, outs, sum_ref = refs[:9], refs[9:13], refs[13]
    extra_s, part_s, top_s, fin_s = refs[14:]
    r = pl.program_id(0)
    remap_step(r, tr_ref.at[r], outs, tabs, extra_s, part_s, top_s, total_cols)

    @pl.when(r == LATE - 1)
    def _():
        me = lax.axis_index(TRC)
        fin_s[...] = close(EARLY, LATE, outs, part_s, top_s, sum_in[...])
        before = jnp.concatenate([fin_s[pl.ds(me ^ t, 1), :] for t in range(4)], axis=0)
        after = jnp.concatenate([fin_s[pl.ds(4 + (me ^ t), 1), :] for t in range(4)], axis=0)
        lane = lax.broadcasted_iota(I32, (4, LANES), 1)
        both = jnp.where(lane < 64, before, pltpu.roll(after, 64, 1))
        for k in range(sum_ref.shape[0]):
            sum_ref[k] = both


WHOLE = pl.BlockSpec(memory_space=pltpu.VMEM)
PARAMS = pltpu.CompilerParams(vmem_limit_bytes=20 * 2**20)


def work(size, cols):
    return [
        pltpu.VMEM((cols // LANES, 4, LANES, LANES), F32),
        pltpu.VMEM((size, 8, LANES), F32),
        pltpu.VMEM((4, cols // LANES, 8, LANES), F32),
    ]


def cost(size):
    return pl.CostEstimate(flops=size * 2_000_000_000, bytes_accessed=size * 1_000_000, transcendentals=0)


def profiles(size, cols):
    return [pltpu.VMEM((size * LEVELS + EXTRA, cols), I16)] * 4


def remap_early(tr, dp, cf, lb, total_cols):
    cols = tr.shape[3]
    nb = cols // LANES
    square = (nb, LANES, LANES)
    outs = profiles(EARLY, cols) + [
        pltpu.VMEM((8, LANES), F32),
        pltpu.VMEM((LATE, 4, LAYERS, cols), BF),
        pltpu.VMEM((LANES, 2 * LANES), BF),
        pltpu.VMEM(square, I32), pltpu.VMEM(square, I32), pltpu.VMEM((nb, 8 * 14, LANES), I32),
        pltpu.VMEM((nb, 8 * 13, LANES), I32), pltpu.VMEM((nb, LEVELS, LANES), I32),
        pltpu.VMEM(square, F32), pltpu.VMEM(square, F32), pltpu.VMEM((nb, LEVELS, LANES), F32),
    ]
    return pl.pallas_call(
        functools.partial(early_kernel, total_cols), grid=(EARLY,),
        in_specs=[
            pl.BlockSpec(memory_space=pltpu.HBM),
            pl.BlockSpec((LAYERS, cols), lambda r: (0, 0)),
            pl.BlockSpec((LEVELS - 1, cols), lambda r: (0, 0)),
            pl.BlockSpec((1, LEVELS, cols), lambda r: (0, 0, 0)),
        ],
        out_specs=[WHOLE] * len(outs), out_shape=outs,
        scratch_shapes=[
            pltpu.VMEM((nb, 136, LANES), I32), pltpu.VMEM((nb, 136, LANES), F32),
            pltpu.VMEM((EARLY, 4, LAYERS, cols), BF), pltpu.SemaphoreType.DMA((EARLY + LATE,)),
        ] + work(EARLY, cols),
        compiler_params=PARAMS, cost_estimate=cost(EARLY), name="remap_early",
    )(tr, dp, cf, lb)


def remap_late(sums, tr, tabs, total_cols, copies):
    cols = tr.shape[3]
    outs = profiles(LATE, cols) + [pltpu.VMEM((copies, 4, LANES), F32)]
    return pl.pallas_call(
        functools.partial(late_kernel, total_cols), grid=(LATE,),
        in_specs=[WHOLE] * 11, out_specs=[WHOLE] * len(outs), out_shape=outs,
        scratch_shapes=work(LATE, cols) + [pltpu.VMEM((8, LANES), F32)],
        compiler_params=PARAMS, cost_estimate=cost(LATE), name="remap_late",
    )(sums, tr, *tabs)


def finish_kernel(meta_ref, *refs, norm):
    codes, (all_ref, out_ref, burden_ref, gain_s) = refs[:8], refs[8:]
    step = pl.program_id(0)
    per = EARLY + LATE

    @pl.when(step == 0)
    def _():
        burden = jnp.sum(all_ref[...], axis=0, keepdims=True) * norm
        burden_ref[...] = burden[0, :per]
        ratio = burden / pltpu.roll(burden, 64, 1)
        gain_s[...] = jnp.broadcast_to(ratio * (1.0 / 65534.0), gain_s.shape)

    for i in range(4):
        @pl.when(step == i)
        def _():
            at = 0
            for ref, size in ((codes[2 * i], EARLY), (codes[2 * i + 1], LATE)):
                tops = jnp.exp2(ref[size * LEVELS:size * LEVELS + EXTRA, :].astype(F32) * (1.0 / 256.0))
                for k in range(size):
                    gain = tops[k:k + 1] * gain_s[0:1, at + k:at + k + 1]
                    code = ref[k * LEVELS:(k + 1) * LEVELS, :].astype(I32) & 65535
                    out_ref[at + k] = (code.astype(F32) * gain).astype(BF)
                at += size


def finish(meta, codes, everyone, norm):
    per, cols = EARLY + LATE, codes[0].shape[1]
    return pl.pallas_call(
        functools.partial(finish_kernel, norm=norm),
        grid_spec=pltpu.PrefetchScalarGridSpec(
            num_scalar_prefetch=1, grid=(4,), in_specs=[WHOLE] * 9,
            out_specs=[pl.BlockSpec((per, LEVELS, cols), lambda s, m: (0, 0, m[0] ^ s)),
                       pl.BlockSpec((per,), lambda s, m: (0,))],
            scratch_shapes=[pltpu.VMEM((8, LANES), F32)]),
        out_shape=[jax.ShapeDtypeStruct((per, LEVELS, 4 * cols), BF),
                   jax.ShapeDtypeStruct((per,), F32)],
        compiler_params=PARAMS, name="finish",
    )(meta, *codes, everyone)


def in_vmem(x):
    return pltpu.with_memory_space_constraint(x, pltpu.VMEM)


def in_hbm(x):
    return pltpu.with_memory_space_constraint(x, pltpu.HBM)


def exchange(part):
    moved = [part[0]]
    for i in range(1, 4):
        moved.append(in_vmem(lax.ppermute(part[i], TRC, [(j, j ^ i) for j in range(4)])))
    return moved


def per_device(tracers_src, layer_dp, cut_frac, level_bounds):
    total_cols = layer_dp.shape[1] * lax.axis_size(COLS_TRC)
    norm = 1.0 / (total_cols * layer_dp.shape[0])
    copies = lax.axis_size(COLS)
    tr = in_hbm(tracers_src.reshape(4, EARLY + LATE, *tracers_src.shape[1:]))
    head = remap_early(tr, in_hbm(layer_dp), in_hbm(cut_frac), in_hbm(level_bounds), total_cols)
    early = exchange(head[:4])
    tail = remap_late(head[4], head[5], head[6:], total_cols, copies)
    everyone = lax.all_to_all(tail[4].reshape(4 * copies, 1, LANES), COLS_TRC, 0, 0, tiled=True)
    late = exchange(tail[:4])
    everyone = in_vmem(everyone.reshape(4 * copies, LANES))
    meta = lax.axis_index(TRC).astype(I32).reshape(1)
    codes = [x for pair in zip(early, late) for x in pair]
    result, burden = finish(meta, codes, everyone, norm)
    return (result, burden)


def solution(mesh):
    split = Mesh(
        mesh.devices.reshape(4, 4, 2, 2, 2), ("cols_0", "cols_1", "cols_2", "trc_0", "trc_1")
    )
    return jax.shard_map(
        per_device,
        mesh=split,
        in_specs=(
            P(None, None, COLS_TRC),
            P(None, COLS_TRC),
            P(None, COLS_TRC),
            P(None, None, COLS_TRC),
        ),
        out_specs=(P(TRC, None, COLS), P(TRC)),
        check_vma=False,
    )
```

time: 211 us -> 43 us (0.20)
  other arithmetic: 55.5 us -> 0 us
  matrix products: 43.1 us -> 0 us
  local copies, waits for them, and re-layouts: 43.1 us -> 0 us
  blocking collectives: 37.2 us -> 0 us
  starting transfers between devices: 4.81 us -> 18.6 us
  waiting for transfers between devices: 25.3 us -> 11.6 us
  Pallas kernels: 0 us -> 12 us
    dot_general x4 -> x0, matrix products: 43.1 us -> none  [remap_block(): jnp.einsum('jsc,qsc->qjc', intersection, layer_mass, precision=lax.Precis...]
    psum x5 -> x0, blocking collectives: 37.2 us -> none  [over_axes(): x = lax.psum(x, axis)]
    reduce_sum x17 -> x0, other arithmetic: 31.3 us -> none  [the longest x4 21.8 us: remap_block(): inner_edges = jnp.sum(intersection * layer_dp[None], axis=1)]
    sub x8 -> x0, other arithmetic: 19.3 us -> none  [the longest x4 18.9 us: remap_block(): remapped = edge_mass[:, 1:] - edge_mass[:, :-1]]
    dynamic_update_slice x16 -> x0, local copies, waits for them, and re-layouts: 14.9 us -> none  [the longest x8 14.6 us: loop_step(): remapped = lax.dynamic_update_slice_in_dim(remapped, block_mass, offset, 2)]
    dynamic_slice x21 -> x0, local copies, waits for them, and re-layouts: 14.1 us -> none  [the longest x20 13.5 us: window(): lax.dynamic_slice_in_dim(values_in, offset, block_cols, values_in.ndim - 1)]
    all_to_all x1, waiting for transfers between devices: 25.3 us -> 11.6 us  [per_device(): lax.all_to_all(tail[4].reshape(4 * copies, 1, LANES), COLS_TRC, 0, 0, til...]
    pallas_call x0 -> x3, Pallas kernels: none -> 12 us  [the longest x1 6.97 us: remap_early(): pl.pallas_call(functools.partial(early_kernel, total_cols), grid=(EARLY,)...]
  transfers between devices with their start and end apart: 1 -> 7, of which waited for: 1 -> 1; matrix products, arithmetic and copies ran while one was open for 0% -> 0% of each run, Pallas kernels for 0% -> 6%
where the time goes in v3:
time: 43 us; the launch traced here: 42.9 us
  starting transfers between devices  18.6 us (43%)
  Pallas kernels  12 us (28%)
  waiting for transfers between devices  11.6 us (27%)
  between operations  0.68 us (2%)
    all_to_all x1, waiting for transfers between devices, per_device(): lax.all_to_all(tail[4].reshape(4 * copies, 1, LANES), COLS_TRC, 0, 0, til...  11.6 us
    all_to_all x1, starting transfers between devices, per_device(): lax.all_to_all(tail[4].reshape(4 * copies, 1, LANES), COLS_TRC, 0, 0, til...  9.45 us
    ppermute x6, starting transfers between devices, exchange(): lax.ppermute(part[i], TRC, [(j, j ^ i) for j in range(4)])  9.12 us
    pallas_call x1, Pallas kernels, remap_early(): pl.pallas_call(functools.partial(early_kernel, total_cols), grid=(EARLY,)...  6.97 us
    pallas_call x1, Pallas kernels, remap_late(): pl.pallas_call(functools.partial(late_kernel, total_cols), grid=(LATE,),...  2.68 us
    pallas_call x1, Pallas kernels, finish(): pl.pallas_call(functools.partial(finish_kernel, norm=norm), grid_spec=plt...  2.35 us
  transfers between devices with their start and end apart: 7, of which 1 were waited for; matrix products, arithmetic and copies ran while one was open for 0% of the time, Pallas kernels for 6%

profile of v3, /device:TPU:1, one launch (start us, length us, event | category | flops | bytes accessed | tf_op | source)
XLA Modules:
  0.0 42.9 jit_solution(14764530415874182637)
XLA Ops:
  0.6 7.0 %remap_early.1 = (s16[368,512]{1,0:T(8,128)(2,1)S(1)}, s16[368,512]{1,0:T(8,128)(2,1)S(1)}, s16[368,512]{1,0:T(8,128)(2,1)S(1)}, s16[368,512]{1,0:T(8,128)(2,1)S...) custom-call(bf16[4,7,127,512]{3,2,1,0:T(8,128)(2,1)} %bitcast.7, ...), custom_call_target="tpu_custom_call" | custom-call | flops 10000000000 | bytes 5000000 | tf_op jit(solution)/shard_map/remap_early/pallas_call | solution.py:265
  7.6 1.5 %collective-permute-start = (s16[368,512]{1,0:T(8,128)(2,1)S(1)}, s16[368,512]{1,0:T(8,128)(2,1)S(1)}, u32[]{:S(2)}, u32[]{:S(2)}) collective-permute-start(s16[368,512]{1,0:T(8,128)(2,1)S(1)} %get-tuple-element.35), channel_id=1, source_target_pairs={{0,1},{1,0},{2,3},{3,2},{4,5},{5,4},{6,7},{7,6},{8,9},{9,8},{10,11... | collective-permute-start | bytes 1130504 | tf_op jit(solution)/shard_map/ppermute | solution.py:344
  9.1 3.0 %collective-permute-start.2 = (s16[368,512]{1,0:T(8,128)(2,1)S(1)}, s16[368,512]{1,0:T(8,128)(2,1)S(1)}, u32[]{:S(2)}, u32[]{:S(2)}) collective-permute-start(s16[368,512]{1,0:T(8,128)(2,1)S(1)} %get-tuple-element.37), channel_id=1, source_target_pairs={{0,2},{1,3},{2,0},{3,1},{4,6},{5,7},{6,4},{7,5},{8,10},{9,11},{10,... | collective-permute-start | bytes 1130504 | tf_op jit(solution)/shard_map/ppermute | solution.py:344
  12.1 0.2 collective-permute-start.4
  12.3 2.7 %remap_late.1 = (s16[152,512]{1,0:T(8,128)(2,1)S(1)}, s16[152,512]{1,0:T(8,128)(2,1)S(1)}, s16[152,512]{1,0:T(8,128)(2,1)}, s16[152,512]{1,0:T(8,128)(2,1)S(1)}, f32[32,4,128]{2,1,0:T(4,128)}) custom-call(f32[8,128]{1,0:T(8,128)S(1)} %get-tuple-element.23.sum_in, bf16[2,4,127,512]{3,2,1,0:T(8,128)(2,1)S(1)} %get-tuple-element.24.tr_ref, ...), custom_call_target="tpu_custom_call" | custom-call | flops 4000000000 | bytes 2000000 | tf_op jit(solution)/shard_map/remap_late/pallas_call | solution.py:285
  15.0 0.2 collective-permute-start.1
  15.2 3.0 %collective-permute-start.3 = (s16[152,512]{1,0:T(8,128)(2,1)}, s16[152,512]{1,0:T(8,128)(2,1)S(1)}, u32[]{:S(2)}, u32[]{:S(2)}) collective-permute-start(s16[152,512]{1,0:T(8,128)(2,1)} %get-tuple-element.38), channel_id=1, source_target_pairs={{0,2},{1,3},{2,0},{3,1},{4,6},{5,7},{6,4},{7,5},{8,10},{9,11},{10,... | collective-permute-start | bytes 466952 | tf_op jit(solution)/shard_map/ppermute | solution.py:344
  18.1 0.0 collective-permute-done.1.refs_3_
  18.1 1.3 %collective-permute-start.5 = (s16[152,512]{1,0:T(8,128)(2,1)S(1)}, s16[152,512]{1,0:T(8,128)(2,1)S(1)}, u32[]{:S(2)}, u32[]{:S(2)}) collective-permute-start(s16[152,512]{1,0:T(8,128)(2,1)S(1)} %get-tuple-element.40), channel_id=1, source_target_pairs={{0,3},{1,2},{2,1},{3,0},{4,7},{5,6},{6,5},{7,4},{8,11},{9,10},{10,... | collective-permute-start | bytes 466952 | tf_op jit(solution)/shard_map/ppermute | solution.py:344
  19.4 9.4 %all-to-all-start = ((f32[128,1,128]{2,1,0:T(1,128)}), f32[128,1,128]{2,1,0:T(1,128)S(1)}, u32[]{:S(2)}, u32[]{:S(2)}) async-start(f32[128,1,128]{2,1,0:T(1,128)} %bitcast.3), calls=%async_computation | async-start | bytes 131072 | tf_op jit(solution)/shard_map/all_to_all | solution.py:356
  28.9 11.6 %all-to-all-done = f32[128,1,128]{2,1,0:T(1,128)S(1)} async-done(((f32[128,1,128]{2,1,0:T(1,128)}), f32[128,1,128]{2,1,0:T(1,128)S(1)}, u32[]{:S(2)}, u32[]{:S(2)}) %all-to-all-start) | async-done | bytes 65568 | tf_op jit(solution)/shard_map/all_to_all | solution.py:356
  40.5 0.0 collective-permute-done.3.refs_5_
  40.5 0.0 collective-permute-done.5.refs_7_
  40.5 0.0 collective-permute-done.refs_2_
  40.5 0.0 collective-permute-done.2.refs_4_
  40.5 0.0 collective-permute-done.4.refs_6_
  40.5 2.3 %finish.1 = (bf16[7,72,2048]{2,1,0:T(8,128)(2,1)}, f32[7]{0:T(128)}) custom-call(s32[1]{0:T(128)} %bitcast.meta_ref, s16[368,512]{1,0:T(8,128)(2,1)S(1)} %get-tuple-element.22.refs_0_, s16[152,512]{1,0:T(8,128)(2,1)S(1)} %get-tuple-element.34.refs_1_, s16[368,512]{1,0:T(8,128)(2,1)S(1)} %collective-permute-done.refs_2_, ...), custom_call_target="tpu_custom_call" | custom-call | tf_op jit(solution)/shard_map/finish/pallas_call | solution.py:320
Async XLA Ops:
  7.6 32.9 %collective-permute-start = (s16[368,512]{1,0:T(8,128)(2,1)S(1)}, s16[368,512]{1,0:T(8,128)(2,1)S(1)}, u32[]{:S(2)}, u32[]{:S(2)}) collective-permute-start(s16[368,512]{1,0:T(8,128)(2,1)S(1)} %get-tuple-element.35), channel_id=1, source_target_pairs={{0,1},{1,0},{2,3},{3,2},{4,5},{5,4},{6,7},{7,6},{8,9},{9,8},{10,11... | collective-permute-start | bytes 1130504 | tf_op jit(solution)/shard_map/ppermute | solution.py:344
  9.1 31.4 %collective-permute-start.2 = (s16[368,512]{1,0:T(8,128)(2,1)S(1)}, s16[368,512]{1,0:T(8,128)(2,1)S(1)}, u32[]{:S(2)}, u32[]{:S(2)}) collective-permute-start(s16[368,512]{1,0:T(8,128)(2,1)S(1)} %get-tuple-element.37), channel_id=1, source_target_pairs={{0,2},{1,3},{2,0},{3,1},{4,6},{5,7},{6,4},{7,5},{8,10},{9,11},{10,... | collective-permute-start | bytes 1130504 | tf_op jit(solution)/shard_map/ppermute | solution.py:344
  12.1 28.4 %collective-permute-start.4 = (s16[368,512]{1,0:T(8,128)(2,1)S(1)}, s16[368,512]{1,0:T(8,128)(2,1)S(1)}, u32[]{:S(2)}, u32[]{:S(2)}) collective-permute-start(s16[368,512]{1,0:T(8,128)(2,1)S(1)} %get-tuple-element.39), channel_id=1, source_target_pairs={{0,3},{1,2},{2,1},{3,0},{4,7},{5,6},{6,5},{7,4},{8,11},{9,10},{10,... | collective-permute-start | bytes 1130504 | tf_op jit(solution)/shard_map/ppermute | solution.py:344
  15.0 3.2 %collective-permute-start.1 = (s16[152,512]{1,0:T(8,128)(2,1)S(1)}, s16[152,512]{1,0:T(8,128)(2,1)S(1)}, u32[]{:S(2)}, u32[]{:S(2)}) collective-permute-start(s16[152,512]{1,0:T(8,128)(2,1)S(1)} %get-tuple-element.36), channel_id=1, source_target_pairs={{0,1},{1,0},{2,3},{3,2},{4,5},{5,4},{6,7},{7,6},{8,9},{9,8},{10,11... | collective-permute-start | bytes 466952 | tf_op jit(solution)/shard_map/ppermute | solution.py:344
  15.2 25.3 %collective-permute-start.3 = (s16[152,512]{1,0:T(8,128)(2,1)}, s16[152,512]{1,0:T(8,128)(2,1)S(1)}, u32[]{:S(2)}, u32[]{:S(2)}) collective-permute-start(s16[152,512]{1,0:T(8,128)(2,1)} %get-tuple-element.38), channel_id=1, source_target_pairs={{0,2},{1,3},{2,0},{3,1},{4,6},{5,7},{6,4},{7,5},{8,10},{9,11},{10,... | collective-permute-start | bytes 466952 | tf_op jit(solution)/shard_map/ppermute | solution.py:344
  18.1 22.3 %collective-permute-start.5 = (s16[152,512]{1,0:T(8,128)(2,1)S(1)}, s16[152,512]{1,0:T(8,128)(2,1)S(1)}, u32[]{:S(2)}, u32[]{:S(2)}) collective-permute-start(s16[152,512]{1,0:T(8,128)(2,1)S(1)} %get-tuple-element.40), channel_id=1, source_target_pairs={{0,3},{1,2},{2,1},{3,0},{4,7},{5,6},{6,5},{7,4},{8,11},{9,10},{10,... | collective-permute-start | bytes 466952 | tf_op jit(solution)/shard_map/ppermute | solution.py:344
  19.4 21.1 %all-to-all-start = ((f32[128,1,128]{2,1,0:T(1,128)}), f32[128,1,128]{2,1,0:T(1,128)S(1)}, u32[]{:S(2)}, u32[]{:S(2)}) async-start(f32[128,1,128]{2,1,0:T(1,128)} %bitcast.3), calls=%async_computation | async-start | bytes 131072 | tf_op jit(solution)/shard_map/all_to_all | solution.py:356

commit v4 on v3

v4 whole, which is shorter than its diff:
```python
import functools
import jax
import jax.numpy as jnp
from jax import lax
from jax.experimental import pallas as pl
from jax.experimental.pallas import tpu as pltpu
from jax.sharding import Mesh
from jax.sharding import PartitionSpec as P

TRC = ("trc_0", "trc_1")
COLS = ("cols_0", "cols_1", "cols_2")
COLS_TRC = ("cols_0", "cols_1", "cols_2", "trc_0", "trc_1")
F32, BF, I32, I16 = jnp.float32, jnp.bfloat16, jnp.int32, jnp.int16
LANES, TILES, OUT = 128, 16, 9
LAYERS, LEVELS, EXTRA = 127, 72, 8
EARLY, LATE = 6, 1

SUBLANE_GATHER = lax.GatherDimensionNumbers(
    offset_dims=(), collapsed_slice_dims=(0,), start_index_map=(0,),
    operand_batching_dims=(1,), start_indices_batching_dims=(1,))


def pick(x, index):
    return lax.gather(x, index[..., None], SUBLANE_GATHER, slice_sizes=(1, 1),
                      mode=lax.GatherScatterMode.PROMISE_IN_BOUNDS)


def tile(x, v):
    return x[8 * v:8 * v + 8]


def row_in_tile():
    return lax.broadcasted_iota(I32, (8, LANES), 0)


def cumulate(tri, mass):
    hi = mass.astype(BF)
    mid = (mass - hi.astype(F32)).astype(BF)
    return jnp.dot(tri[...], jnp.concatenate([hi, mid], axis=0), preferred_element_type=F32)


def edge_differences(cum, extra, cb, idx_s, over_s, one_s, two_s, four_s):
    n = len(cum)
    row8 = row_in_tile()
    y = [[None] * 15 for _ in range(n)]
    z = [[None] * 15 for _ in range(n)]
    w = [[None] * 13 for _ in range(n)]
    edge = [[None] * OUT for _ in range(n)]
    roll = [[None] * OUT for _ in range(n)]
    diff = [[None] * OUT for _ in range(n)]
    point = [tile(cum[i], 0) + extra(i, 0) for i in range(n)]
    for v in range(15):
        ix = idx_s[cb, 8 * v:8 * v + 8, :]
        over = over_s[cb, 8 * v:8 * v + 8, :] != 0
        for i in range(n):
            nxt = tile(cum[i], v + 1) + extra(i, v + 1)
            y[i][v] = jnp.where(over, pick(nxt, ix), pick(point[i], ix))
            point[i] = nxt
        a = v - 1
        if a >= 0:
            m = one_s[cb, 8 * a:8 * a + 8, :] != 0
            for i in range(n):
                z[i][a] = jnp.where(m, y[i][a + 1], y[i][a])
        if v == 14:
            for i in range(n):
                z[i][14] = y[i][14]
        for b in ([v - 3] if v < 14 else [11, 12]):
            if b < 0:
                continue
            m = two_s[cb, 8 * b:8 * b + 8, :] != 0
            for i in range(n):
                w[i][b] = jnp.where(m, z[i][b + 2], z[i][b])
            o = b - 4
            if o < 0:
                continue
            m = four_s[cb, 8 * o:8 * o + 8, :] != 0
            for i in range(n):
                edge[i][o] = jnp.where(m, w[i][o + 4], w[i][o])
                roll[i][o] = pltpu.roll(edge[i][o], 7, 0)
                if o > 0:
                    diff[i][o - 1] = jnp.where(row8 == 7, roll[i][o], roll[i][o - 1]) - edge[i][o - 1]
    for i in range(n):
        total = jnp.broadcast_to(cum[i][LAYERS:LAYERS + 1], (8, LANES))
        diff[i][OUT - 1] = jnp.where(row8 == 7, total, roll[i][OUT - 1]) - edge[i][OUT - 1]
    return diff


def prepare(dp_ref, cf_ref, lb_ref, tri, idx_s, over_s, one_s, two_s, four_s, dp_s, psi_s, inv_s, dbuf, fbuf):
    rr = lax.broadcasted_iota(I32, (LANES, 2 * LANES), 0)
    cc = lax.broadcasted_iota(I32, (LANES, 2 * LANES), 1) & (LANES - 1)
    tri[...] = (cc < rr).astype(F32).astype(BF)
    row8 = row_in_tile()
    zero_i, zero_f = jnp.zeros((8, LANES), I32), jnp.zeros((8, LANES), F32)
    for cb in range(dp_s.shape[0]):
        dbuf[cb, 0:8, :] = zero_i
        fbuf[cb, 0:8, :] = zero_f
        at = slice(cb * LANES, (cb + 1) * LANES)
        d = lb_ref[0, :, at] - lax.broadcasted_iota(I32, (LEVELS, LANES), 0)
        high, low = d >> 3, d & 7
        f = jnp.concatenate([jnp.zeros((1, LANES), F32), cf_ref[:, at]], axis=0)
        for v in range(TILES):
            dv, fv = zero_i, zero_f
            for h in range(7):
                if 0 <= v - h < OUT:
                    m = tile(high, v - h) == h
                    dv = jnp.where(m, tile(low, v - h), dv)
                    fv = jnp.where(m, tile(f, v - h), fv)
            dbuf[cb, 8 + 8 * v:16 + 8 * v, :] = dv
            fbuf[cb, 8 + 8 * v:16 + 8 * v, :] = fv
            t = row8 + dv
            idx_s[cb, 8 * v:8 * v + 8, :] = t & 7
            over_s[cb, 8 * v:8 * v + 8, :] = t >> 3
        for v in range(14):
            bit = zero_i
            for h in (0, 2, 4, 6):
                if 0 <= v - h < OUT:
                    bit = jnp.where(tile(high, v - h) == h + 1, 1, bit)
            one_s[cb, 8 * v:8 * v + 8, :] = bit
        for v in range(13):
            bit = zero_i
            for h in (0, 4):
                if 0 <= v - h < OUT:
                    bit = jnp.where((tile(high, v - h) >> 1) == (h >> 1) + 1, 1, bit)
            two_s[cb, 8 * v:8 * v + 8, :] = bit
        four_s[cb] = high >> 2
        phi = jnp.zeros((LANES, LANES), F32)
        for k in range(8):
            phi = phi + jnp.where(dbuf[cb, 8 - k:136 - k, :] == k, fbuf[cb, 8 - k:136 - k, :], 0.0)
        dp = jnp.concatenate([dp_ref[:, at], jnp.zeros((1, LANES), F32)], axis=0)
        psi = phi * dp
        dp_s[cb] = dp
        psi_s[cb] = psi
        (thick,) = edge_differences(
            [cumulate(tri, dp)], lambda i, v: tile(psi, v), cb, idx_s, over_s, one_s, two_s, four_s)
        for o in range(OUT):
            inv_s[cb, 8 * o:8 * o + 8, :] = 1.0 / thick[o]


def half_step(r, pair, load, outs, row, tabs, extra_s, part, top_s, total_cols):
    tri, idx_s, over_s, one_s, two_s, four_s, dp_s, psi_s, inv_s = tabs
    blocks = dp_s.shape[0]
    start = (lax.axis_index(COLS) * lax.axis_size(TRC) + lax.axis_index(TRC)) * blocks * LANES
    before, after = [None] * 2, [None] * 2
    for cb in range(blocks):
        at = slice(cb * LANES, (cb + 1) * LANES)
        position = start + cb * LANES + lax.broadcasted_iota(I32, (1, LANES), 1)
        area = 1.0 + 2.0 * position.astype(F32) / total_cols
        mass = []
        for i in range(2):
            t = jnp.concatenate([load(i, at).astype(F32), jnp.zeros((1, LANES), F32)], axis=0)
            mass.append(t * dp_s[cb])
            extra_s[cb, i] = t * psi_s[cb]
        both = cumulate(tri, jnp.concatenate(mass, axis=1))
        cum = [both[:, :LANES], both[:, LANES:]]
        diff = edge_differences(
            cum, lambda i, v: extra_s[cb, i, 8 * v:8 * v + 8, :], cb, idx_s, over_s, one_s, two_s, four_s)
        for i in range(2):
            kept = [jnp.maximum(x, 0.0) for x in diff[i]]
            mean = [kept[o] * inv_s[cb, 8 * o:8 * o + 8, :] for o in range(OUT)]
            sums, top = kept[0], mean[0]
            for o in range(1, OUT):
                sums, top = sums + kept[o], jnp.maximum(top, mean[o])
            top = jnp.max(top, axis=0, keepdims=True)
            step = jnp.ceil(jnp.log2(jnp.maximum(top, 1e-33)) * 256.0)
            scale = 65534.0 / jnp.exp2(step * (1.0 / 256.0))
            code = jnp.concatenate([(x * scale + 0.5).astype(I32) for x in mean], axis=0)
            outs[i][pl.ds(pl.multiple_of(row * LEVELS, 8), LEVELS), at] = code.astype(I16)
            top_s[i, cb, pl.ds(row, 1), :] = step
            last, area_sum = cum[i][LAYERS:LAYERS + 1] * area, sums * area
            before[i] = last if cb == 0 else before[i] + last
            after[i] = area_sum if cb == 0 else after[i] + area_sum
    for i in range(2):
        part[r, pair + i:pair + i + 1, :] = before[i]
        part[r, 4 + pair + i:5 + pair + i, :] = jnp.sum(after[i], axis=0, keepdims=True)


def write_tops(size, outs, top_s):
    for i in range(2):
        tops = jnp.concatenate([top_s[i, c] for c in range(top_s.shape[1])], axis=1)
        outs[i][size * LEVELS:size * LEVELS + EXTRA, :] = tops.astype(I32).astype(I16)


def early_kernel(total_cols, tr_hbm, dp_ref, cf_ref, lb_ref, *refs):
    outs, part, near_ref, far_ref, tabs = refs[:2], refs[2], refs[3], refs[4], refs[5:14]
    dbuf, fbuf, held, sems, extra_s, top_s = refs[14:]
    me = lax.axis_index(TRC)
    near = (me >> 1) * 2
    far = 2 - near
    odd = me & 1
    copies = [
        pltpu.make_async_copy(
            tr_hbm.at[pl.ds(far, 2), r], held.at[r] if r < EARLY else far_ref.at[r - EARLY], sems.at[r])
        for r in range(EARLY + LATE)]
    rest = pltpu.make_async_copy(tr_hbm.at[pl.ds(near, 2)], near_ref, sems.at[EARLY + LATE])
    for c in copies[:2]:
        c.start()
    prepare(dp_ref, cf_ref, lb_ref, *tabs, dbuf, fbuf)
    for c in copies[2:]:
        c.start()
    rest.start()

    def steps(g, carry):
        for h in range(2):
            r = 2 * g + h
            pltpu.make_async_copy(tr_hbm.at[pl.ds(far, 2), r], held.at[r], sems.at[r]).wait()
        for h in range(2):
            r = 2 * g + h
            half_step(r, 2, lambda i, at: held[r, odd ^ i, :, at], outs, r, tabs, extra_s.at[h], part, top_s, total_cols)
        return carry

    lax.fori_loop(0, EARLY // 2, steps, 0)
    write_tops(EARLY, outs, top_s)
    for c in copies[EARLY:]:
        c.wait()
    rest.wait()


def late_kernel(total_cols, early_part, near_ref, far_ref, *refs):
    tabs, near_outs, far_outs, sum_ref = refs[:9], refs[9:11], refs[11:13], refs[13]
    extra_s, top_near, top_far, part, fin_s = refs[14:]
    me = lax.axis_index(TRC)
    odd = me & 1
    per = EARLY + LATE

    def near_step(r, h):
        half_step(r, 0, lambda i, at: near_ref[odd ^ i, r, :, at], near_outs, r, tabs,
                  extra_s.at[h], part, top_near, total_cols)

    def steps(g, carry):
        for h in range(2):
            near_step(2 * g + h, h)
        return carry

    lax.fori_loop(0, per // 2, steps, 0)
    near_step(per - 1, 0)
    half_step(EARLY, 2, lambda i, at: far_ref[0, odd ^ i, :, at], far_outs, 0, tabs,
              extra_s.at[1], part, top_far, total_cols)
    write_tops(LATE, far_outs, top_far)
    write_tops(per, near_outs, top_near)
    lane = lax.broadcasted_iota(I32, (8, LANES), 1)
    theirs = (lax.broadcasted_iota(I32, (8, LANES), 0) & 2) != 0
    acc = jnp.zeros((8, LANES), F32)
    for r in range(per):
        p = jnp.where(theirs, early_part[r], part[r]) if r < EARLY else part[r]
        acc = jnp.where(lane == r, jnp.sum(p, axis=1, keepdims=True), acc)
    fin_s[...] = acc
    before = jnp.concatenate([fin_s[pl.ds(me ^ t, 1), :] for t in range(4)], axis=0)
    after = jnp.concatenate([fin_s[pl.ds(4 + (me ^ t), 1), :] for t in range(4)], axis=0)
    lane = lax.broadcasted_iota(I32, (4, LANES), 1)
    both = jnp.where(lane < 64, before, pltpu.roll(after, 64, 1))
    for k in range(sum_ref.shape[0]):
        sum_ref[k] = both


WHOLE = pl.BlockSpec(memory_space=pltpu.VMEM)
PARAMS = pltpu.CompilerParams(vmem_limit_bytes=20 * 2**20)


def cost(size):
    return pl.CostEstimate(flops=size * 1_000_000_000, bytes_accessed=size * 500_000, transcendentals=0)


def profiles(size, cols):
    return [pltpu.VMEM((size * LEVELS + EXTRA, cols), I16)] * 2


def remap_early(tr, dp, cf, lb, total_cols):
    cols = tr.shape[3]
    nb = cols // LANES
    per = EARLY + LATE
    square = (nb, LANES, LANES)
    outs = profiles(EARLY, cols) + [
        pltpu.VMEM((EARLY, 8, LANES), F32),
        pltpu.VMEM((2, per, LAYERS, cols), BF),
        pltpu.VMEM((LATE, 2, LAYERS, cols), BF),
        pltpu.VMEM((LANES, 2 * LANES), BF),
        pltpu.VMEM(square, I32), pltpu.VMEM(square, I32), pltpu.VMEM((nb, 8 * 14, LANES), I32),
        pltpu.VMEM((nb, 8 * 13, LANES), I32), pltpu.VMEM((nb, LEVELS, LANES), I32),
        pltpu.VMEM(square, F32), pltpu.VMEM(square, F32), pltpu.VMEM((nb, LEVELS, LANES), F32),
    ]
    return pl.pallas_call(
        functools.partial(early_kernel, total_cols), grid=(1,),
        in_specs=[
            pl.BlockSpec(memory_space=pltpu.HBM),
            pl.BlockSpec((LAYERS, cols), lambda r: (0, 0)),
            pl.BlockSpec((LEVELS - 1, cols), lambda r: (0, 0)),
            pl.BlockSpec((1, LEVELS, cols), lambda r: (0, 0, 0)),
        ],
        out_specs=[WHOLE] * len(outs), out_shape=outs,
        scratch_shapes=[
            pltpu.VMEM((nb, 136, LANES), I32), pltpu.VMEM((nb, 136, LANES), F32),
            pltpu.VMEM((EARLY, 2, LAYERS, cols), BF), pltpu.SemaphoreType.DMA((per + 1,)),
            pltpu.VMEM((2, nb, 2, LANES, LANES), F32), pltpu.VMEM((2, nb, 8, LANES), F32),
        ],
        compiler_params=PARAMS, cost_estimate=cost(EARLY), name="remap_early",
    )(tr, dp, cf, lb)


def remap_late(part, near, far, tabs, total_cols, copies):
    cols = near.shape[3]
    nb = cols // LANES
    per = EARLY + LATE
    outs = profiles(per, cols) + profiles(LATE, cols) + [pltpu.VMEM((copies, 4, LANES), F32)]
    return pl.pallas_call(
        functools.partial(late_kernel, total_cols), grid=(1,),
        in_specs=[WHOLE] * 12, out_specs=[WHOLE] * len(outs), out_shape=outs,
        scratch_shapes=[
            pltpu.VMEM((2, nb, 2, LANES, LANES), F32), pltpu.VMEM((2, nb, 8, LANES), F32),
            pltpu.VMEM((2, nb, 8, LANES), F32), pltpu.VMEM((per, 8, LANES), F32), pltpu.VMEM((8, LANES), F32),
        ],
        compiler_params=PARAMS, cost_estimate=cost(per + LATE), name="remap_late",
    )(part, near, far, *tabs)


def finish_kernel(*refs, norm):
    near0, near1, early2, early3, late2, late3, all_ref, out_hbm, burden_ref, buf, sems = refs
    per = EARLY + LATE
    me = lax.axis_index(TRC)
    cols = near0.shape[1]
    burden = jnp.sum(all_ref[...], axis=0, keepdims=True) * norm
    burden_ref[...] = burden[0, :per]
    ratio = burden / pltpu.roll(burden, 64, 1) * (1.0 / 65534.0)
    groups = (((near0, per),), ((near1, per),), ((early2, EARLY), (late2, LATE)), ((early3, EARLY), (late3, LATE)))
    tops = [[(ref, k, jnp.exp2(ref[size * LEVELS:size * LEVELS + EXTRA, :].astype(F32) * (1.0 / 256.0))[k:k + 1])
             for ref, size in parts for k in range(size)] for parts in groups]
    copies = []
    for r in range(per):
        for i in range(4):
            ref, k, top = tops[i][r]
            at = pl.ds(pl.multiple_of((me ^ i) * cols, cols), cols)
            code = ref[k * LEVELS:(k + 1) * LEVELS, :].astype(I32) & 65535
            buf[r, :, at] = (code.astype(F32) * (top * ratio[0:1, r:r + 1])).astype(BF)
        copies.append(pltpu.make_async_copy(buf.at[r], out_hbm.at[r], sems.at[r]))
        copies[-1].start()
    for c in copies:
        c.wait()


def finish(codes, everyone, norm):
    per, cols = EARLY + LATE, codes[0].shape[1]
    return pl.pallas_call(
        functools.partial(finish_kernel, norm=norm), grid=(1,),
        in_specs=[WHOLE] * 7,
        out_specs=[pl.BlockSpec(memory_space=pltpu.HBM), pl.BlockSpec((per,), lambda s: (0,))],
        scratch_shapes=[pltpu.VMEM((per, LEVELS, 4 * cols), BF), pltpu.SemaphoreType.DMA((per,))],
        out_shape=[jax.ShapeDtypeStruct((per, LEVELS, 4 * cols), BF),
                   jax.ShapeDtypeStruct((per,), F32)],
        compiler_params=PARAMS, name="finish",
    )(*codes, everyone)


def in_vmem(x):
    return pltpu.with_memory_space_constraint(x, pltpu.VMEM)


def in_hbm(x):
    return pltpu.with_memory_space_constraint(x, pltpu.HBM)


def swap(x, i):
    return in_vmem(lax.ppermute(x, TRC, [(j, j ^ i) for j in range(4)]))


def per_device(tracers_src, layer_dp, cut_frac, level_bounds):
    total_cols = layer_dp.shape[1] * lax.axis_size(COLS_TRC)
    norm = 1.0 / (total_cols * layer_dp.shape[0])
    copies = lax.axis_size(COLS)
    tr = in_hbm(tracers_src.reshape(4, EARLY + LATE, *tracers_src.shape[1:]))
    head = remap_early(tr, in_hbm(layer_dp), in_hbm(cut_frac), in_hbm(level_bounds), total_cols)
    early = [swap(head[i], 2 + i) for i in range(2)]
    tail = remap_late(head[2], head[3], head[4], head[5:], total_cols, copies)
    everyone = lax.all_to_all(tail[4].reshape(4 * copies, 1, LANES), COLS_TRC, 0, 0, tiled=True)
    near = [tail[0], swap(tail[1], 1)]
    late = [swap(tail[2 + i], 2 + i) for i in range(2)]
    everyone = in_vmem(everyone.reshape(4 * copies, LANES))
    return tuple(finish(near + early + late, everyone, norm))


def solution(mesh):
    split = Mesh(
        mesh.devices.reshape(4, 4, 2, 2, 2), ("cols_0", "cols_1", "cols_2", "trc_0", "trc_1")
    )
    return jax.shard_map(
        per_device,
        mesh=split,
        in_specs=(
            P(None, None, COLS_TRC),
            P(None, COLS_TRC),
            P(None, COLS_TRC),
            P(None, None, COLS_TRC),
        ),
        out_specs=(P(TRC, None, COLS), P(TRC)),
        check_vma=False,
    )
```

time: 43 us -> 44.9 us (1.044)
  blocking collectives: 0 us -> 24.8 us
  waiting for transfers between devices: 11.6 us -> 0.01 us
  starting transfers between devices: 18.6 us -> 8.02 us
  Pallas kernels: 12 us -> 11.3 us
    all_to_all x0 -> x1, blocking collectives: none -> 24.8 us  [per_device(): lax.all_to_all(tail[4].reshape(4 * copies, 1, LANES), COLS_TRC, 0, 0, til...]
    all_to_all x1 -> x0, waiting for transfers between devices: 11.6 us -> none  [per_device(): lax.all_to_all(tail[4].reshape(4 * copies, 1, LANES), COLS_TRC, 0, 0, til...]
    all_to_all x1 -> x0, starting transfers between devices: 9.45 us -> none  [per_device(): lax.all_to_all(tail[4].reshape(4 * copies, 1, LANES), COLS_TRC, 0, 0, til...]
    ppermute x6 -> x5, starting transfers between devices: 9.12 us -> 8.02 us  [swap(): return in_vmem(lax.ppermute(x, TRC, [(j, j ^ i) for j in range(4)]))]
    pallas_call x3, Pallas kernels: 12 us -> 11.3 us  [the longest x1 5.19 us: remap_early(): pl.pallas_call(functools.partial(early_kernel, total_cols), grid=(1,), in...]
  transfers between devices with their start and end apart: 7 -> 5, of which waited for: 1 -> 0; matrix products, arithmetic and copies ran while one was open for 0% -> 0% of each run, Pallas kernels for 6% -> 0%
where the time goes in v4:
time: 44.9 us; the launch traced here: 44.8 us
  blocking collectives  24.8 us (55%)
  Pallas kernels  11.3 us (25%)
  starting transfers between devices  8.02 us (18%)
  between operations  0.66 us (1%)
    all_to_all x1, blocking collectives, per_device(): lax.all_to_all(tail[4].reshape(4 * copies, 1, LANES), COLS_TRC, 0, 0, til...  24.8 us
    ppermute x5, starting transfers between devices, swap(): return in_vmem(lax.ppermute(x, TRC, [(j, j ^ i) for j in range(4)]))  8.02 us
    pallas_call x1, Pallas kernels, remap_early(): pl.pallas_call(functools.partial(early_kernel, total_cols), grid=(1,), in...  5.19 us
    pallas_call x1, Pallas kernels, remap_late(): pl.pallas_call(functools.partial(late_kernel, total_cols), grid=(1,), in_...  3.99 us
    pallas_call x1, Pallas kernels, finish(): pl.pallas_call(functools.partial(finish_kernel, norm=norm), grid=(1,), in...  2.09 us
  transfers between devices with their start and end apart: 5, of which 0 were waited for; matrix products, arithmetic and copies ran while one was open for 0% of the time, Pallas kernels for 0%

profile of v4, /device:TPU:1, one launch (start us, length us, event | category | flops | bytes accessed | tf_op | source)
XLA Modules:
  0.0 44.8 jit_solution(2828233852069438460)
XLA Ops:
  0.6 5.2 %remap_early.1 = (s16[440,512]{1,0:T(8,128)(2,1)S(1)}, s16[440,512]{1,0:T(8,128)(2,1)S(1)}, f32[6,8,128]{2,1,0:T(8,128)S(1)}, bf16[2,7,127,512]{3,2,1,0:T(8,128)...) custom-call(bf16[4,7,127,512]{3,2,1,0:T(8,128)(2,1)} %bitcast.7, ...), custom_call_target="tpu_custom_call" | custom-call | flops 6000000000 | bytes 3000000 | tf_op jit(solution)/shard_map/remap_early/pallas_call | solution.py:281
  5.8 4.0 %remap_late.1 = (s16[512,512]{1,0:T(8,128)(2,1)S(1)}, s16[512,512]{1,0:T(8,128)(2,1)S(1)}, s16[80,512]{1,0:T(8,128)(2,1)S(1)}, s16[80,512]{1,0:T(8,128)(2,1)S(1)}, f32[32,4,128]{2,1,0:T(4,128)S(1)}) custom-call(f32[6,8,128]{2,1,0:T(8,128)S(1)} %get-tuple-element.21.early_part, bf16[2,7,127,512]{3,2,1,0:T(8,128)(2,1)S(1)} %get-tuple-element.22.near_ref, ...), custom_call_target="tpu_custom_call" | custom-call | flops 8000000000 | bytes 4000000 | tf_op jit(solution)/shard_map/remap_late/pallas_call | solution.py:304
  9.8 1.5 %collective-permute-start = (s16[512,512]{1,0:T(8,128)(2,1)S(1)}, s16[512,512]{1,0:T(8,128)(2,1)S(1)}, u32[]{:S(2)}, u32[]{:S(2)}) collective-permute-start(s16[512,512]{1,0:T(8,128)(2,1)S(1)} %get-tuple-element.34), channel_id=1, source_target_pairs={{0,1},{1,0},{2,3},{3,2},{4,5},{5,4},{6,7},{7,6},{8,9},{9,8},{10,11... | collective-permute-start | bytes 1572872 | tf_op jit(solution)/shard_map/ppermute | solution.py:361
  11.3 3.0 %collective-permute-start.1 = (s16[440,512]{1,0:T(8,128)(2,1)S(1)}, s16[440,512]{1,0:T(8,128)(2,1)S(1)}, u32[]{:S(2)}, u32[]{:S(2)}) collective-permute-start(s16[440,512]{1,0:T(8,128)(2,1)S(1)} %get-tuple-element.35), channel_id=1, source_target_pairs={{0,2},{1,3},{2,0},{3,1},{4,6},{5,7},{6,4},{7,5},{8,10},{9,11},{10,... | collective-permute-start | bytes 1351688 | tf_op jit(solution)/shard_map/ppermute | solution.py:361
  14.3 0.2 collective-permute-start.2
  14.5 3.0 %collective-permute-start.3 = (s16[80,512]{1,0:T(8,128)(2,1)S(1)}, s16[80,512]{1,0:T(8,128)(2,1)S(1)}, u32[]{:S(2)}, u32[]{:S(2)}) collective-permute-start(s16[80,512]{1,0:T(8,128)(2,1)S(1)} %get-tuple-element.37), channel_id=1, source_target_pairs={{0,2},{1,3},{2,0},{3,1},{4,6},{5,7},{6,4},{7,5},{8,10},{9,11},{10,... | collective-permute-start | bytes 245768 | tf_op jit(solution)/shard_map/ppermute | solution.py:361
  17.5 0.3 collective-permute-start.4
  17.8 24.8 %all_to_all.5 = f32[128,1,128]{2,1,0:T(1,128)S(1)} all-to-all(f32[128,1,128]{2,1,0:T(1,128)S(1)} %bitcast.6), channel_id=1, replica_groups=mesh['cols_0'=4,'cols_1'=4,'cols_2'=2,'trc_0'=2,'trc_1'=2] {'cols_0','co..., dimensions={0} | all-to-all | bytes 131072 | tf_op jit(solution)/shard_map/all_to_all | solution.py:372
  42.6 0.0 collective-permute-done.3.refs_4_
  42.7 0.0 collective-permute-done.4.refs_5_
  42.7 0.0 collective-permute-done.1.refs_2_
  42.7 0.0 collective-permute-done.2.refs_3_
  42.7 0.0 collective-permute-done.refs_1_
  42.7 2.1 %finish.1 = (bf16[7,72,2048]{2,1,0:T(8,128)(2,1)}, f32[7]{0:T(128)}) custom-call(s16[512,512]{1,0:T(8,128)(2,1)S(1)} %get-tuple-element.33.refs_0_, s16[512,512]{1,0:T(8,128)(2,1)S(1)} %collective-permute-done.refs_1_, s16[440,512]{1,0:T(8,128)(2,1)S(1)} %collective-permute-done.1.refs_2_, s16[440,512]{1,0:T(8,128)(2,1)S(1)} %collective-permute-done.2.refs_3_, ...), custom_call_target="tpu_custom_call" | custom-call | tf_op jit(solution)/shard_map/finish/pallas_call | solution.py:341
Async XLA Ops:
  9.8 32.9 %collective-permute-start = (s16[512,512]{1,0:T(8,128)(2,1)S(1)}, s16[512,512]{1,0:T(8,128)(2,1)S(1)}, u32[]{:S(2)}, u32[]{:S(2)}) collective-permute-start(s16[512,512]{1,0:T(8,128)(2,1)S(1)} %get-tuple-element.34), channel_id=1, source_target_pairs={{0,1},{1,0},{2,3},{3,2},{4,5},{5,4},{6,7},{7,6},{8,9},{9,8},{10,11... | collective-permute-start | bytes 1572872 | tf_op jit(solution)/shard_map/ppermute | solution.py:361
  11.3 31.4 %collective-permute-start.1 = (s16[440,512]{1,0:T(8,128)(2,1)S(1)}, s16[440,512]{1,0:T(8,128)(2,1)S(1)}, u32[]{:S(2)}, u32[]{:S(2)}) collective-permute-start(s16[440,512]{1,0:T(8,128)(2,1)S(1)} %get-tuple-element.35), channel_id=1, source_target_pairs={{0,2},{1,3},{2,0},{3,1},{4,6},{5,7},{6,4},{7,5},{8,10},{9,11},{10,... | collective-permute-start | bytes 1351688 | tf_op jit(solution)/shard_map/ppermute | solution.py:361
  14.3 28.4 %collective-permute-start.2 = (s16[440,512]{1,0:T(8,128)(2,1)S(1)}, s16[440,512]{1,0:T(8,128)(2,1)S(1)}, u32[]{:S(2)}, u32[]{:S(2)}) collective-permute-start(s16[440,512]{1,0:T(8,128)(2,1)S(1)} %get-tuple-element.36), channel_id=1, source_target_pairs={{0,3},{1,2},{2,1},{3,0},{4,7},{5,6},{6,5},{7,4},{8,11},{9,10},{10,... | collective-permute-start | bytes 1351688 | tf_op jit(solution)/shard_map/ppermute | solution.py:361
  14.5 28.2 %collective-permute-start.3 = (s16[80,512]{1,0:T(8,128)(2,1)S(1)}, s16[80,512]{1,0:T(8,128)(2,1)S(1)}, u32[]{:S(2)}, u32[]{:S(2)}) collective-permute-start(s16[80,512]{1,0:T(8,128)(2,1)S(1)} %get-tuple-element.37), channel_id=1, source_target_pairs={{0,2},{1,3},{2,0},{3,1},{4,6},{5,7},{6,4},{7,5},{8,10},{9,11},{10,... | collective-permute-start | bytes 245768 | tf_op jit(solution)/shard_map/ppermute | solution.py:361
  17.5 25.1 %collective-permute-start.4 = (s16[80,512]{1,0:T(8,128)(2,1)S(1)}, s16[80,512]{1,0:T(8,128)(2,1)S(1)}, u32[]{:S(2)}, u32[]{:S(2)}) collective-permute-start(s16[80,512]{1,0:T(8,128)(2,1)S(1)} %get-tuple-element.38), channel_id=1, source_target_pairs={{0,3},{1,2},{2,1},{3,0},{4,7},{5,6},{6,5},{7,4},{8,11},{9,10},{10,... | collective-permute-start | bytes 245768 | tf_op jit(solution)/shard_map/ppermute | solution.py:361

commit v5 on v4

--- a/solution.py
+++ b/solution.py
@@ -136,53 +136,70 @@
             inv_s[cb, 8 * o:8 * o + 8, :] = 1.0 / thick[o]
 
 
-def half_step(r, pair, load, outs, row, tabs, extra_s, part, top_s, total_cols):
+def encode(outs, row, top_s):
+    def sink(i, cb, at, mean):
+        top = mean[0]
+        for o in range(1, OUT):
+            top = jnp.maximum(top, mean[o])
+        step, scale = unit(jnp.max(top, axis=0, keepdims=True))
+        code = jnp.concatenate([(x * scale + 0.5).astype(I32) for x in mean], axis=0)
+        outs[i][pl.ds(pl.multiple_of(row * LEVELS, 8), LEVELS), at] = code.astype(I16)
+        top_s[i, cb, pl.ds(row, 1), :] = step
+
+    return sink
+
+
+def unit(top):
+    step = jnp.ceil(jnp.log2(jnp.maximum(top, 1e-33)) * 256.0)
+    return step, 65534.0 / jnp.exp2(step * (1.0 / 256.0))
+
+
+def half_steps(jobs, tabs, extra_s, part, total_cols):
     tri, idx_s, over_s, one_s, two_s, four_s, dp_s, psi_s, inv_s = tabs
     blocks = dp_s.shape[0]
     start = (lax.axis_index(COLS) * lax.axis_size(TRC) + lax.axis_index(TRC)) * blocks * LANES
-    before, after = [None] * 2, [None] * 2
+    before, after = {}, {}
     for cb in range(blocks):
         at = slice(cb * LANES, (cb + 1) * LANES)
         position = start + cb * LANES + lax.broadcasted_iota(I32, (1, LANES), 1)
         area = 1.0 + 2.0 * position.astype(F32) / total_cols
-        mass = []
+        for h, (_, _, load, sink) in enumerate(jobs):
+            mass = []
+            for i in range(2):
+                t = jnp.concatenate([load(i, at).astype(F32), jnp.zeros((1, LANES), F32)], axis=0)
+                mass.append(t * dp_s[cb])
+                extra_s[h, cb, i] = t * psi_s[cb]
+            both = cumulate(tri, jnp.concatenate(mass, axis=1))
+            cum = [both[:, :LANES], both[:, LANES:]]
+            diff = edge_differences(
+                cum, lambda i, v: extra_s[h, cb, i, 8 * v:8 * v + 8, :], cb, idx_s, over_s, one_s, two_s, four_s)
+            for i in range(2):
+                kept = [jnp.maximum(x, 0.0) for x in diff[i]]
+                sums = kept[0]
+                for o in range(1, OUT):
+                    sums = sums + kept[o]
+                sink(i, cb, at, [kept[o] * inv_s[cb, 8 * o:8 * o + 8, :] for o in range(OUT)])
+                last, area_sum = cum[i][LAYERS:LAYERS + 1] * area, sums * area
+                before[h, i] = last if cb == 0 else before[h, i] + last
+                after[h, i] = area_sum if cb == 0 else after[h, i] + area_sum
+    for h, (r, pair, _, _) in enumerate(jobs):
         for i in range(2):
-            t = jnp.concatenate([load(i, at).astype(F32), jnp.zeros((1, LANES), F32)], axis=0)
-            mass.append(t * dp_s[cb])
-            extra_s[cb, i] = t * psi_s[cb]
-        both = cumulate(tri, jnp.concatenate(mass, axis=1))
-        cum = [both[:, :LANES], both[:, LANES:]]
-        diff = edge_differences(
-            cum, lambda i, v: extra_s[cb, i, 8 * v:8 * v + 8, :], cb, idx_s, over_s, one_s, two_s, four_s)
-        for i in range(2):
-            kept = [jnp.maximum(x, 0.0) for x in diff[i]]
-            mean = [kept[o] * inv_s[cb, 8 * o:8 * o + 8, :] for o in range(OUT)]
-            sums, top = kept[0], mean[0]
-            for o in range(1, OUT):
-                sums, top = sums + kept[o], jnp.maximum(top, mean[o])
-            top = jnp.max(top, axis=0, keepdims=True)
-            step = jnp.ceil(jnp.log2(jnp.maximum(top, 1e-33)) * 256.0)
-            scale = 65534.0 / jnp.exp2(step * (1.0 / 256.0))
-            code = jnp.concatenate([(x * scale + 0.5).astype(I32) for x in mean], axis=0)
-            outs[i][pl.ds(pl.multiple_of(row * LEVELS, 8), LEVELS), at] = code.astype(I16)
-            top_s[i, cb, pl.ds(row, 1), :] = step
-            last, area_sum = cum[i][LAYERS:LAYERS + 1] * area, sums * area
-            before[i] = last if cb == 0 else before[i] + last
-            after[i] = area_sum if cb == 0 else after[i] + area_sum
-    for i in range(2):
-        part[r, pair + i:pair + i + 1, :] = before[i]
-        part[r, 4 + pair + i:5 + pair + i, :] = jnp.sum(after[i], axis=0, keepdims=True)
+            part[r, pair + i:pair + i + 1, :] = before[h, i]
+            part[r, 4 + pair + i:5 + pair + i, :] = jnp.sum(after[h, i], axis=0, keepdims=True)
 
 
 def write_tops(size, outs, top_s):
     for i in range(2):
+        if outs[i] is None:
+            continue
         tops = jnp.concatenate([top_s[i, c] for c in range(top_s.shape[1])], axis=1)
         outs[i][size * LEVELS:size * LEVELS + EXTRA, :] = tops.astype(I32).astype(I16)
 
 
 def early_kernel(total_cols, tr_hbm, dp_ref, cf_ref, lb_ref, *refs):
-    outs, part, near_ref, far_ref, tabs = refs[:2], refs[2], refs[3], refs[4], refs[5:14]
-    dbuf, fbuf, held, sems, extra_s, top_s = refs[14:]
+    result, part, near_ref, far_ref, tabs = refs[:2], refs[2], refs[3], refs[4], refs[5:14]
+    dbuf, fbuf, held, sems, extra_s, top_s, out_a, out_b, out_sems = refs[14:]
+    outs = (out_a, out_b)
     me = lax.axis_index(TRC)
     near = (me >> 1) * 2
     far = 2 - near
@@ -199,17 +216,36 @@
         c.start()
     rest.start()
 
+    def written(g):
+        rows = pl.ds(pl.multiple_of(2 * g * LEVELS, 16), 2 * LEVELS)
+        return [
+            pltpu.make_async_copy(outs[i].at[rows, :], result[i].at[rows, :], out_sems.at[2 * g + i]) for i in range(2)]
+
     def steps(g, carry):
         for h in range(2):
             r = 2 * g + h
             pltpu.make_async_copy(tr_hbm.at[pl.ds(far, 2), r], held.at[r], sems.at[r]).wait()
-        for h in range(2):
-            r = 2 * g + h
-            half_step(r, 2, lambda i, at: held[r, odd ^ i, :, at], outs, r, tabs, extra_s.at[h], part, top_s, total_cols)
+        half_steps(
+            [(2 * g + h, 2, lambda i, at, h=h: held[2 * g + h, odd ^ i, :, at], encode(outs, 2 * g + h, top_s))
+             for h in range(2)], tabs, extra_s, part, total_cols)
+        for c in written(g):
+            c.start()
         return carry
 
     lax.fori_loop(0, EARLY // 2, steps, 0)
     write_tops(EARLY, outs, top_s)
+    last = [
+        pltpu.make_async_copy(
+            outs[i].at[EARLY * LEVELS:EARLY * LEVELS + EXTRA, :], result[i].at[EARLY * LEVELS:EARLY * LEVELS + EXTRA, :],
+            out_sems.at[EARLY + i])
+        for i in range(2)]
+    for c in last:
+        c.start()
+    for g in range(EARLY // 2):
+        for c in written(g):
+            c.wait()
+    for c in last:
+        c.wait()
     for c in copies[EARLY:]:
         c.wait()
     rest.wait()
@@ -222,21 +258,26 @@
     odd = me & 1
     per = EARLY + LATE
 
-    def near_step(r, h):
-        half_step(r, 0, lambda i, at: near_ref[odd ^ i, r, :, at], near_outs, r, tabs,
-                  extra_s.at[h], part, top_near, total_cols)
+    def near_job(r):
+        code = encode((None, near_outs[1]), r, top_near)
+
+        def sink(i, cb, at, mean):
+            if i == 0:
+                near_outs[0][r, :, at] = jnp.concatenate(mean, axis=0)
+            else:
+                code(i, cb, at, mean)
+
+        return (r, 0, lambda i, at: near_ref[odd ^ i, r, :, at], sink)
 
     def steps(g, carry):
-        for h in range(2):
-            near_step(2 * g + h, h)
+        half_steps([near_job(2 * g), near_job(2 * g + 1)], tabs, extra_s, part, total_cols)
         return carry
 
     lax.fori_loop(0, per // 2, steps, 0)
-    near_step(per - 1, 0)
-    half_step(EARLY, 2, lambda i, at: far_ref[0, odd ^ i, :, at], far_outs, 0, tabs,
-              extra_s.at[1], part, top_far, total_cols)
+    far_job = (EARLY, 2, lambda i, at: far_ref[0, odd ^ i, :, at], encode(far_outs, 0, top_far))
+    half_steps([near_job(per - 1), far_job], tabs, extra_s, part, total_cols)
     write_tops(LATE, far_outs, top_far)
-    write_tops(per, near_outs, top_near)
+    write_tops(per, (None, near_outs[1]), top_near)
     lane = lax.broadcasted_iota(I32, (8, LANES), 1)
     theirs = (lax.broadcasted_iota(I32, (8, LANES), 0) & 2) != 0
     acc = jnp.zeros((8, LANES), F32)
@@ -269,7 +310,7 @@
     nb = cols // LANES
     per = EARLY + LATE
     square = (nb, LANES, LANES)
-    outs = profiles(EARLY, cols) + [
+    outs = [jax.ShapeDtypeStruct((EARLY * LEVELS + EXTRA, cols), I16)] * 2 + [
         pltpu.VMEM((EARLY, 8, LANES), F32),
         pltpu.VMEM((2, per, LAYERS, cols), BF),
         pltpu.VMEM((LATE, 2, LAYERS, cols), BF),
@@ -286,12 +327,12 @@
             pl.BlockSpec((LEVELS - 1, cols), lambda r: (0, 0)),
             pl.BlockSpec((1, LEVELS, cols), lambda r: (0, 0, 0)),
         ],
-        out_specs=[WHOLE] * len(outs), out_shape=outs,
+        out_specs=[pl.BlockSpec(memory_space=pltpu.HBM)] * 2 + [WHOLE] * (len(outs) - 2), out_shape=outs,
         scratch_shapes=[
             pltpu.VMEM((nb, 136, LANES), I32), pltpu.VMEM((nb, 136, LANES), F32),
             pltpu.VMEM((EARLY, 2, LAYERS, cols), BF), pltpu.SemaphoreType.DMA((per + 1,)),
             pltpu.VMEM((2, nb, 2, LANES, LANES), F32), pltpu.VMEM((2, nb, 8, LANES), F32),
-        ],
+        ] + profiles(EARLY, cols) + [pltpu.SemaphoreType.DMA((EARLY + 2,))],
         compiler_params=PARAMS, cost_estimate=cost(EARLY), name="remap_early",
     )(tr, dp, cf, lb)
 
@@ -300,10 +341,12 @@
     cols = near.shape[3]
     nb = cols // LANES
     per = EARLY + LATE
-    outs = profiles(per, cols) + profiles(LATE, cols) + [pltpu.VMEM((copies, 4, LANES), F32)]
+    outs = [pltpu.VMEM((per, LEVELS, cols), F32), profiles(per, cols)[0]] + profiles(LATE, cols)
+    outs += [jax.ShapeDtypeStruct((copies, 4, LANES), F32)]
     return pl.pallas_call(
         functools.partial(late_kernel, total_cols), grid=(1,),
-        in_specs=[WHOLE] * 12, out_specs=[WHOLE] * len(outs), out_shape=outs,
+        in_specs=[WHOLE] * 12,
+        out_specs=[WHOLE] * 4 + [pl.BlockSpec((copies, 4, LANES), lambda g: (0, 0, 0))], out_shape=outs,
         scratch_shapes=[
             pltpu.VMEM((2, nb, 2, LANES, LANES), F32), pltpu.VMEM((2, nb, 8, LANES), F32),
             pltpu.VMEM((2, nb, 8, LANES), F32), pltpu.VMEM((per, 8, LANES), F32), pltpu.VMEM((8, LANES), F32),
@@ -316,17 +359,20 @@
     near0, near1, early2, early3, late2, late3, all_ref, out_hbm, burden_ref, buf, sems = refs
     per = EARLY + LATE
     me = lax.axis_index(TRC)
-    cols = near0.shape[1]
+    cols = near1.shape[1]
     burden = jnp.sum(all_ref[...], axis=0, keepdims=True) * norm
     burden_ref[...] = burden[0, :per]
-    ratio = burden / pltpu.roll(burden, 64, 1) * (1.0 / 65534.0)
-    groups = (((near0, per),), ((near1, per),), ((early2, EARLY), (late2, LATE)), ((early3, EARLY), (late3, LATE)))
+    plain = burden / pltpu.roll(burden, 64, 1)
+    ratio = plain * (1.0 / 65534.0)
+    groups = (((near1, per),), ((early2, EARLY), (late2, LATE)), ((early3, EARLY), (late3, LATE)))
     tops = [[(ref, k, jnp.exp2(ref[size * LEVELS:size * LEVELS + EXTRA, :].astype(F32) * (1.0 / 256.0))[k:k + 1])
              for ref, size in parts for k in range(size)] for parts in groups]
     copies = []
     for r in range(per):
-        for i in range(4):
-            ref, k, top = tops[i][r]
+        own = pl.ds(pl.multiple_of(me * cols, cols), cols)
+        buf[r, :, own] = (near0[r] * plain[0:1, r:r + 1]).astype(BF)
+        for i in range(1, 4):
+            ref, k, top = tops[i - 1][r]
             at = pl.ds(pl.multiple_of((me ^ i) * cols, cols), cols)
             code = ref[k * LEVELS:(k + 1) * LEVELS, :].astype(I32) & 65535
             buf[r, :, at] = (code.astype(F32) * (top * ratio[0:1, r:r + 1])).astype(BF)
@@ -337,7 +383,7 @@
 
 
 def finish(codes, everyone, norm):
-    per, cols = EARLY + LATE, codes[0].shape[1]
+    per, cols = EARLY + LATE, codes[1].shape[1]
     return pl.pallas_call(
         functools.partial(finish_kernel, norm=norm), grid=(1,),
         in_specs=[WHOLE] * 7,

time: 44.9 us -> 45.5 us (1.013)
  Pallas kernels: 11.3 us -> 11.8 us
    pallas_call x1, Pallas kernels: 5.19 us -> 6.24 us  [remap_early(): pl.pallas_call(functools.partial(early_kernel, total_cols), grid=(1,), in...]
    pallas_call x1, Pallas kernels: 3.99 us -> 3.5 us  [remap_late(): pl.pallas_call(functools.partial(late_kernel, total_cols), grid=(1,), in_...]
where the time goes in v5:
time: 45.5 us; the launch traced here: 45.4 us
  blocking collectives  24.8 us (55%)
  Pallas kernels  11.8 us (26%)
  starting transfers between devices  8.02 us (18%)
  between operations  0.66 us (1%)
    all_to_all x1, blocking collectives, per_device(): lax.all_to_all(tail[4].reshape(4 * copies, 1, LANES), COLS_TRC, 0, 0, til...  24.8 us
    ppermute x5, starting transfers between devices, swap(): return in_vmem(lax.ppermute(x, TRC, [(j, j ^ i) for j in range(4)]))  8.02 us
    pallas_call x1, Pallas kernels, remap_early(): pl.pallas_call(functools.partial(early_kernel, total_cols), grid=(1,), in...  6.24 us
    pallas_call x1, Pallas kernels, remap_late(): pl.pallas_call(functools.partial(late_kernel, total_cols), grid=(1,), in_...  3.5 us
    pallas_call x1, Pallas kernels, finish(): pl.pallas_call(functools.partial(finish_kernel, norm=norm), grid=(1,), in...  2.1 us
  transfers between devices with their start and end apart: 5, of which 0 were waited for; matrix products, arithmetic and copies ran while one was open for 0% of the time, Pallas kernels for 0%

profile of v5, /device:TPU:1, one launch (start us, length us, event | category | flops | bytes accessed | tf_op | source)
XLA Modules:
  0.0 45.4 jit_solution(9125728955585163861)
XLA Ops:
  0.6 6.2 %remap_early.1 = (s16[440,512]{1,0:T(8,128)(2,1)S(1)}, s16[440,512]{1,0:T(8,128)(2,1)S(1)}, f32[6,8,128]{2,1,0:T(8,128)S(1)}, bf16[2,7,127,512]{3,2,1,0:T(8,128)...) custom-call(bf16[4,7,127,512]{3,2,1,0:T(8,128)(2,1)} %bitcast.7, ...), custom_call_target="tpu_custom_call" | custom-call | flops 6000000000 | bytes 3000000 | tf_op jit(solution)/shard_map/remap_early/pallas_call | solution.py:322
  6.9 3.5 %remap_late.1 = (f32[7,72,512]{2,1,0:T(8,128)S(1)}, s16[512,512]{1,0:T(8,128)(2,1)S(1)}, s16[80,512]{1,0:T(8,128)(2,1)S(1)}, s16[80,512]{1,0:T(8,128)(2,1)S(1)}, f32[32,4,128]{2,1,0:T(4,128)S(1)}) custom-call(f32[6,8,128]{2,1,0:T(8,128)S(1)} %get-tuple-element.21.early_part, bf16[2,7,127,512]{3,2,1,0:T(8,128)(2,1)S(1)} %get-tuple-element.22.near_ref, ...), custom_call_target="tpu_custom_call" | custom-call | flops 8000000000 | bytes 4000000 | tf_op jit(solution)/shard_map/remap_late/pallas_call | solution.py:346
  10.4 1.5 %collective-permute-start = (s16[512,512]{1,0:T(8,128)(2,1)S(1)}, s16[512,512]{1,0:T(8,128)(2,1)S(1)}, u32[]{:S(2)}, u32[]{:S(2)}) collective-permute-start(s16[512,512]{1,0:T(8,128)(2,1)S(1)} %get-tuple-element.34), channel_id=1, source_target_pairs={{0,1},{1,0},{2,3},{3,2},{4,5},{5,4},{6,7},{7,6},{8,9},{9,8},{10,11... | collective-permute-start | bytes 1572872 | tf_op jit(solution)/shard_map/ppermute | solution.py:407
  11.8 3.0 %collective-permute-start.1 = (s16[440,512]{1,0:T(8,128)(2,1)S(1)}, s16[440,512]{1,0:T(8,128)(2,1)S(1)}, u32[]{:S(2)}, u32[]{:S(2)}) collective-permute-start(s16[440,512]{1,0:T(8,128)(2,1)S(1)} %get-tuple-element.35), channel_id=1, source_target_pairs={{0,2},{1,3},{2,0},{3,1},{4,6},{5,7},{6,4},{7,5},{8,10},{9,11},{10,... | collective-permute-start | bytes 1351688 | tf_op jit(solution)/shard_map/ppermute | solution.py:407
  14.9 0.2 collective-permute-start.2
  15.1 3.0 %collective-permute-start.3 = (s16[80,512]{1,0:T(8,128)(2,1)S(1)}, s16[80,512]{1,0:T(8,128)(2,1)S(1)}, u32[]{:S(2)}, u32[]{:S(2)}) collective-permute-start(s16[80,512]{1,0:T(8,128)(2,1)S(1)} %get-tuple-element.37), channel_id=1, source_target_pairs={{0,2},{1,3},{2,0},{3,1},{4,6},{5,7},{6,4},{7,5},{8,10},{9,11},{10,... | collective-permute-start | bytes 245768 | tf_op jit(solution)/shard_map/ppermute | solution.py:407
  18.1 0.3 collective-permute-start.4
  18.4 24.8 %all_to_all.5 = f32[128,1,128]{2,1,0:T(1,128)S(1)} all-to-all(f32[128,1,128]{2,1,0:T(1,128)S(1)} %bitcast.6), channel_id=1, replica_groups=mesh['cols_0'=4,'cols_1'=4,'cols_2'=2,'trc_0'=2,'trc_1'=2] {'cols_0','co..., dimensions={0} | all-to-all | bytes 131072 | tf_op jit(solution)/shard_map/all_to_all | solution.py:418
  43.2 0.0 collective-permute-done.3.refs_4_
  43.2 0.0 collective-permute-done.4.refs_5_
  43.2 0.0 collective-permute-done.1.refs_2_
  43.2 0.0 collective-permute-done.2.refs_3_
  43.2 0.0 collective-permute-done.refs_1_
  43.3 2.1 %finish.1 = (bf16[7,72,2048]{2,1,0:T(8,128)(2,1)}, f32[7]{0:T(128)}) custom-call(f32[7,72,512]{2,1,0:T(8,128)S(1)} %get-tuple-element.33.refs_0_, s16[512,512]{1,0:T(8,128)(2,1)S(1)} %collective-permute-done.refs_1_, s16[440,512]{1,0:T(8,128)(2,1)S(1)} %collective-permute-done.1.refs_2_, s16[440,512]{1,0:T(8,128)(2,1)S(1)} %collective-permute-done.2.refs_3_, ...), custom_call_target="tpu_custom_call" | custom-call | tf_op jit(solution)/shard_map/finish/pallas_call | solution.py:387
Async XLA Ops:
  10.4 32.9 %collective-permute-start = (s16[512,512]{1,0:T(8,128)(2,1)S(1)}, s16[512,512]{1,0:T(8,128)(2,1)S(1)}, u32[]{:S(2)}, u32[]{:S(2)}) collective-permute-start(s16[512,512]{1,0:T(8,128)(2,1)S(1)} %get-tuple-element.34), channel_id=1, source_target_pairs={{0,1},{1,0},{2,3},{3,2},{4,5},{5,4},{6,7},{7,6},{8,9},{9,8},{10,11... | collective-permute-start | bytes 1572872 | tf_op jit(solution)/shard_map/ppermute | solution.py:407
  11.8 31.4 %collective-permute-start.1 = (s16[440,512]{1,0:T(8,128)(2,1)S(1)}, s16[440,512]{1,0:T(8,128)(2,1)S(1)}, u32[]{:S(2)}, u32[]{:S(2)}) collective-permute-start(s16[440,512]{1,0:T(8,128)(2,1)S(1)} %get-tuple-element.35), channel_id=1, source_target_pairs={{0,2},{1,3},{2,0},{3,1},{4,6},{5,7},{6,4},{7,5},{8,10},{9,11},{10,... | collective-permute-start | bytes 1351688 | tf_op jit(solution)/shard_map/ppermute | solution.py:407
  14.9 28.4 %collective-permute-start.2 = (s16[440,512]{1,0:T(8,128)(2,1)S(1)}, s16[440,512]{1,0:T(8,128)(2,1)S(1)}, u32[]{:S(2)}, u32[]{:S(2)}) collective-permute-start(s16[440,512]{1,0:T(8,128)(2,1)S(1)} %get-tuple-element.36), channel_id=1, source_target_pairs={{0,3},{1,2},{2,1},{3,0},{4,7},{5,6},{6,5},{7,4},{8,11},{9,10},{10,... | collective-permute-start | bytes 1351688 | tf_op jit(solution)/shard_map/ppermute | solution.py:407
  15.1 28.2 %collective-permute-start.3 = (s16[80,512]{1,0:T(8,128)(2,1)S(1)}, s16[80,512]{1,0:T(8,128)(2,1)S(1)}, u32[]{:S(2)}, u32[]{:S(2)}) collective-permute-start(s16[80,512]{1,0:T(8,128)(2,1)S(1)} %get-tuple-element.37), channel_id=1, source_target_pairs={{0,2},{1,3},{2,0},{3,1},{4,6},{5,7},{6,4},{7,5},{8,10},{9,11},{10,... | collective-permute-start | bytes 245768 | tf_op jit(solution)/shard_map/ppermute | solution.py:407
  18.1 25.1 %collective-permute-start.4 = (s16[80,512]{1,0:T(8,128)(2,1)S(1)}, s16[80,512]{1,0:T(8,128)(2,1)S(1)}, u32[]{:S(2)}, u32[]{:S(2)}) collective-permute-start(s16[80,512]{1,0:T(8,128)(2,1)S(1)} %get-tuple-element.38), channel_id=1, source_target_pairs={{0,3},{1,2},{2,1},{3,0},{4,7},{5,6},{6,5},{7,4},{8,11},{9,10},{10,... | collective-permute-start | bytes 245768 | tf_op jit(solution)/shard_map/ppermute | solution.py:407

commit v6 on v5

--- a/solution.py
+++ b/solution.py
@@ -13,7 +13,7 @@
 F32, BF, I32, I16 = jnp.float32, jnp.bfloat16, jnp.int32, jnp.int16
 LANES, TILES, OUT = 128, 16, 9
 LAYERS, LEVELS, EXTRA = 127, 72, 8
-EARLY, LATE = 6, 1
+EARLY, LATE, KEPT = 6, 1, 5
 
 SUBLANE_GATHER = lax.GatherDimensionNumbers(
     offset_dims=(), collapsed_slice_dims=(0,), start_index_map=(0,),
@@ -197,8 +197,8 @@
 
 
 def early_kernel(total_cols, tr_hbm, dp_ref, cf_ref, lb_ref, *refs):
-    result, part, near_ref, far_ref, tabs = refs[:2], refs[2], refs[3], refs[4], refs[5:14]
-    dbuf, fbuf, held, sems, extra_s, top_s, out_a, out_b, out_sems = refs[14:]
+    result, part, near_ref, far_ref, tabs, spare = refs[:2], refs[2], refs[3], refs[4], refs[5:14], refs[14]
+    dbuf, fbuf, held, sems, extra_s, top_s, out_a, out_b, out_sems = refs[15:]
     outs = (out_a, out_b)
     me = lax.axis_index(TRC)
     near = (me >> 1) * 2
@@ -228,21 +228,24 @@
         half_steps(
             [(2 * g + h, 2, lambda i, at, h=h: held[2 * g + h, odd ^ i, :, at], encode(outs, 2 * g + h, top_s))
              for h in range(2)], tabs, extra_s, part, total_cols)
-        for c in written(g):
-            c.start()
+        both = written(g)
+        both[0].start()
+        pl.when(g < EARLY // 2 - 1)(both[1].start)
         return carry
 
     lax.fori_loop(0, EARLY // 2, steps, 0)
     write_tops(EARLY, outs, top_s)
+    ends = ((EARLY * LEVELS, EARLY * LEVELS, EXTRA), (EARLY * LEVELS, KEPT * LEVELS, EXTRA))
+    ends += ((2 * (EARLY // 2 - 1) * LEVELS, 2 * (EARLY // 2 - 1) * LEVELS, LEVELS),)
     last = [
         pltpu.make_async_copy(
-            outs[i].at[EARLY * LEVELS:EARLY * LEVELS + EXTRA, :], result[i].at[EARLY * LEVELS:EARLY * LEVELS + EXTRA, :],
-            out_sems.at[EARLY + i])
-        for i in range(2)]
+            outs[min(i, 1)].at[a:a + n, :], result[min(i, 1)].at[b:b + n, :], out_sems.at[EARLY + i])
+        for i, (a, b, n) in enumerate(ends)]
     for c in last:
         c.start()
+    spare[...] = out_b[KEPT * LEVELS:EARLY * LEVELS, :]
     for g in range(EARLY // 2):
-        for c in written(g):
+        for c in written(g)[:2 if g < EARLY // 2 - 1 else 1]:
             c.wait()
     for c in last:
         c.wait()
@@ -251,7 +254,7 @@
     rest.wait()
 
 
-def late_kernel(total_cols, early_part, near_ref, far_ref, *refs):
+def late_kernel(total_cols, early_part, near_ref, far_ref, spare, *refs):
     tabs, near_outs, far_outs, sum_ref = refs[:9], refs[9:11], refs[11:13], refs[13]
     extra_s, top_near, top_far, part, fin_s = refs[14:]
     me = lax.axis_index(TRC)
@@ -277,6 +280,7 @@
     far_job = (EARLY, 2, lambda i, at: far_ref[0, odd ^ i, :, at], encode(far_outs, 0, top_far))
     half_steps([near_job(per - 1), far_job], tabs, extra_s, part, total_cols)
     write_tops(LATE, far_outs, top_far)
+    far_outs[1][LATE * LEVELS + EXTRA:, :] = spare[...]
     write_tops(per, (None, near_outs[1]), top_near)
     lane = lax.broadcasted_iota(I32, (8, LANES), 1)
     theirs = (lax.broadcasted_iota(I32, (8, LANES), 0) & 2) != 0
@@ -310,7 +314,7 @@
     nb = cols // LANES
     per = EARLY + LATE
     square = (nb, LANES, LANES)
-    outs = [jax.ShapeDtypeStruct((EARLY * LEVELS + EXTRA, cols), I16)] * 2 + [
+    outs = [jax.ShapeDtypeStruct((n * LEVELS + EXTRA, cols), I16) for n in (EARLY, KEPT)] + [
         pltpu.VMEM((EARLY, 8, LANES), F32),
         pltpu.VMEM((2, per, LAYERS, cols), BF),
         pltpu.VMEM((LATE, 2, LAYERS, cols), BF),
@@ -318,6 +322,7 @@
         pltpu.VMEM(square, I32), pltpu.VMEM(square, I32), pltpu.VMEM((nb, 8 * 14, LANES), I32),
         pltpu.VMEM((nb, 8 * 13, LANES), I32), pltpu.VMEM((nb, LEVELS, LANES), I32),
         pltpu.VMEM(square, F32), pltpu.VMEM(square, F32), pltpu.VMEM((nb, LEVELS, LANES), F32),
+        pltpu.VMEM((LEVELS, cols), I16),
     ]
     return pl.pallas_call(
         functools.partial(early_kernel, total_cols), grid=(1,),
@@ -332,27 +337,28 @@
             pltpu.VMEM((nb, 136, LANES), I32), pltpu.VMEM((nb, 136, LANES), F32),
             pltpu.VMEM((EARLY, 2, LAYERS, cols), BF), pltpu.SemaphoreType.DMA((per + 1,)),
             pltpu.VMEM((2, nb, 2, LANES, LANES), F32), pltpu.VMEM((2, nb, 8, LANES), F32),
-        ] + profiles(EARLY, cols) + [pltpu.SemaphoreType.DMA((EARLY + 2,))],
+        ] + profiles(EARLY, cols) + [pltpu.SemaphoreType.DMA((EARLY + 3,))],
         compiler_params=PARAMS, cost_estimate=cost(EARLY), name="remap_early",
     )(tr, dp, cf, lb)
 
 
-def remap_late(part, near, far, tabs, total_cols, copies):
+def remap_late(part, near, far, spare, tabs, total_cols, copies):
     cols = near.shape[3]
     nb = cols // LANES
     per = EARLY + LATE
-    outs = [pltpu.VMEM((per, LEVELS, cols), F32), profiles(per, cols)[0]] + profiles(LATE, cols)
+    outs = [pltpu.VMEM((per, LEVELS, cols), F32), profiles(per, cols)[0], profiles(LATE, cols)[0]]
+    outs += [pltpu.VMEM(((LATE + 1) * LEVELS + EXTRA, cols), I16)]
     outs += [jax.ShapeDtypeStruct((copies, 4, LANES), F32)]
     return pl.pallas_call(
         functools.partial(late_kernel, total_cols), grid=(1,),
-        in_specs=[WHOLE] * 12,
+        in_specs=[WHOLE] * 13,
         out_specs=[WHOLE] * 4 + [pl.BlockSpec((copies, 4, LANES), lambda g: (0, 0, 0))], out_shape=outs,
         scratch_shapes=[
             pltpu.VMEM((2, nb, 2, LANES, LANES), F32), pltpu.VMEM((2, nb, 8, LANES), F32),
             pltpu.VMEM((2, nb, 8, LANES), F32), pltpu.VMEM((per, 8, LANES), F32), pltpu.VMEM((8, LANES), F32),
         ],
         compiler_params=PARAMS, cost_estimate=cost(per + LATE), name="remap_late",
-    )(part, near, far, *tabs)
+    )(part, near, far, spare, *tabs)
 
 
 def finish_kernel(*refs, norm):
@@ -364,9 +370,16 @@
     burden_ref[...] = burden[0, :per]
     plain = burden / pltpu.roll(burden, 64, 1)
     ratio = plain * (1.0 / 65534.0)
-    groups = (((near1, per),), ((early2, EARLY), (late2, LATE)), ((early3, EARLY), (late3, LATE)))
-    tops = [[(ref, k, jnp.exp2(ref[size * LEVELS:size * LEVELS + EXTRA, :].astype(F32) * (1.0 / 256.0))[k:k + 1])
-             for ref, size in parts for k in range(size)] for parts in groups]
+
+    def tops_of(ref, size):
+        return jnp.exp2(ref[size * LEVELS:size * LEVELS + EXTRA, :].astype(F32) * (1.0 / 256.0))
+
+    near_top, top2, top3 = tops_of(near1, per), tops_of(early2, EARLY), tops_of(early3, KEPT)
+    end2, end3 = tops_of(late2, LATE), tops_of(late3, LATE)
+    tops = [[(near1, k * LEVELS, near_top[k:k + 1]) for k in range(per)],
+            [(early2, k * LEVELS, top2[k:k + 1]) for k in range(EARLY)] + [(late2, 0, end2[0:1])],
+            [(early3, k * LEVELS, top3[k:k + 1]) for k in range(KEPT)]
+            + [(late3, LATE * LEVELS + EXTRA, top3[KEPT:EARLY]), (late3, 0, end3[0:1])]]
     copies = []
     for r in range(per):
         own = pl.ds(pl.multiple_of(me * cols, cols), cols)
@@ -374,7 +387,7 @@
         for i in range(1, 4):
             ref, k, top = tops[i - 1][r]
             at = pl.ds(pl.multiple_of((me ^ i) * cols, cols), cols)
-            code = ref[k * LEVELS:(k + 1) * LEVELS, :].astype(I32) & 65535
+            code = ref[k:k + LEVELS, :].astype(I32) & 65535
             buf[r, :, at] = (code.astype(F32) * (top * ratio[0:1, r:r + 1])).astype(BF)
         copies.append(pltpu.make_async_copy(buf.at[r], out_hbm.at[r], sems.at[r]))
         copies[-1].start()
@@ -414,7 +427,7 @@
     tr = in_hbm(tracers_src.reshape(4, EARLY + LATE, *tracers_src.shape[1:]))
     head = remap_early(tr, in_hbm(layer_dp), in_hbm(cut_frac), in_hbm(level_bounds), total_cols)
     early = [swap(head[i], 2 + i) for i in range(2)]
-    tail = remap_late(head[2], head[3], head[4], head[5:], total_cols, copies)
+    tail = remap_late(head[2], head[3], head[4], head[14], head[5:14], total_cols, copies)
     everyone = lax.all_to_all(tail[4].reshape(4 * copies, 1, LANES), COLS_TRC, 0, 0, tiled=True)
     near = [tail[0], swap(tail[1], 1)]
     late = [swap(tail[2 + i], 2 + i) for i in range(2)]

time: 45.5 us -> 45.4 us (level)
  no operation moved by 1% of the time
where the time goes in v6:
time: 45.4 us; the launch traced here: 45.3 us
  blocking collectives  25.1 us (55%)
  Pallas kernels  11.7 us (26%)
  starting transfers between devices  7.74 us (17%)
  between operations  0.66 us (1%)
    all_to_all x1, blocking collectives, per_device(): lax.all_to_all(tail[4].reshape(4 * copies, 1, LANES), COLS_TRC, 0, 0, til...  25.1 us
    ppermute x5, starting transfers between devices, swap(): return in_vmem(lax.ppermute(x, TRC, [(j, j ^ i) for j in range(4)]))  7.74 us
    pallas_call x1, Pallas kernels, remap_early(): pl.pallas_call(functools.partial(early_kernel, total_cols), grid=(1,), in...  6.16 us
    pallas_call x1, Pallas kernels, remap_late(): pl.pallas_call(functools.partial(late_kernel, total_cols), grid=(1,), in_...  3.49 us
    pallas_call x1, Pallas kernels, finish(): pl.pallas_call(functools.partial(finish_kernel, norm=norm), grid=(1,), in...  2.1 us
  transfers between devices with their start and end apart: 5, of which 0 were waited for; matrix products, arithmetic and copies ran while one was open for 0% of the time, Pallas kernels for 0%

profile of v6, /device:TPU:1, one launch (start us, length us, event | category | flops | bytes accessed | tf_op | source)
XLA Modules:
  0.0 45.3 jit_solution(17356379355412754401)
XLA Ops:
  0.6 6.2 %remap_early.1 = (s16[440,512]{1,0:T(8,128)(2,1)S(1)}, s16[368,512]{1,0:T(8,128)(2,1)S(1)}, f32[6,8,128]{2,1,0:T(8,128)S(1)}, bf16[2,7,127,512]{3,2,1,0:T(8,128)...) custom-call(bf16[4,7,127,512]{3,2,1,0:T(8,128)(2,1)} %bitcast.7, ...), custom_call_target="tpu_custom_call" | custom-call | flops 6000000000 | bytes 3000000 | tf_op jit(solution)/shard_map/remap_early/pallas_call | solution.py:327
  6.8 3.5 %remap_late.1 = (f32[7,72,512]{2,1,0:T(8,128)S(1)}, s16[512,512]{1,0:T(8,128)(2,1)S(1)}, s16[80,512]{1,0:T(8,128)(2,1)S(1)}, s16[152,512]{1,0:T(8,128)(2,1)S(1)}, f32[32,4,128]{2,1,0:T(4,128)S(1)}) custom-call(f32[6,8,128]{2,1,0:T(8,128)S(1)} %get-tuple-element.22.early_part, bf16[2,7,127,512]{3,2,1,0:T(8,128)(2,1)S(1)} %get-tuple-element.23.near_ref, ...), custom_call_target="tpu_custom_call" | custom-call | flops 8000000000 | bytes 4000000 | tf_op jit(solution)/shard_map/remap_late/pallas_call | solution.py:352
  10.3 1.5 %collective-permute-start = (s16[512,512]{1,0:T(8,128)(2,1)S(1)}, s16[512,512]{1,0:T(8,128)(2,1)S(1)}, u32[]{:S(2)}, u32[]{:S(2)}) collective-permute-start(s16[512,512]{1,0:T(8,128)(2,1)S(1)} %get-tuple-element.36), channel_id=1, source_target_pairs={{0,1},{1,0},{2,3},{3,2},{4,5},{5,4},{6,7},{7,6},{8,9},{9,8},{10,11... | collective-permute-start | bytes 1572872 | tf_op jit(solution)/shard_map/ppermute | solution.py:420
  11.7 3.0 %collective-permute-start.1 = (s16[440,512]{1,0:T(8,128)(2,1)S(1)}, s16[440,512]{1,0:T(8,128)(2,1)S(1)}, u32[]{:S(2)}, u32[]{:S(2)}) collective-permute-start(s16[440,512]{1,0:T(8,128)(2,1)S(1)} %get-tuple-element.37), channel_id=1, source_target_pairs={{0,2},{1,3},{2,0},{3,1},{4,6},{5,7},{6,4},{7,5},{8,10},{9,11},{10,... | collective-permute-start | bytes 1351688 | tf_op jit(solution)/shard_map/ppermute | solution.py:420
  14.8 0.2 collective-permute-start.2
  15.0 3.0 %collective-permute-start.4 = (s16[152,512]{1,0:T(8,128)(2,1)S(1)}, s16[152,512]{1,0:T(8,128)(2,1)S(1)}, u32[]{:S(2)}, u32[]{:S(2)}) collective-permute-start(s16[152,512]{1,0:T(8,128)(2,1)S(1)} %get-tuple-element.40), channel_id=1, source_target_pairs={{0,3},{1,2},{2,1},{3,0},{4,7},{5,6},{6,5},{7,4},{8,11},{9,10},{10,... | collective-permute-start | bytes 466952 | tf_op jit(solution)/shard_map/ppermute | solution.py:420
  18.0 0.0 collective-permute-start.3
  18.0 25.1 %all_to_all.5 = f32[128,1,128]{2,1,0:T(1,128)S(1)} all-to-all(f32[128,1,128]{2,1,0:T(1,128)S(1)} %bitcast.6), channel_id=1, replica_groups=mesh['cols_0'=4,'cols_1'=4,'cols_2'=2,'trc_0'=2,'trc_1'=2] {'cols_0','co..., dimensions={0} | all-to-all | bytes 131072 | tf_op jit(solution)/shard_map/all_to_all | solution.py:431
  43.1 0.0 collective-permute-done.3.refs_4_
  43.1 0.0 collective-permute-done.4.refs_5_
  43.1 0.0 collective-permute-done.2.refs_3_
  43.1 0.0 collective-permute-done.1.refs_2_
  43.1 0.0 collective-permute-done.refs_1_
  43.2 2.1 %finish.1 = (bf16[7,72,2048]{2,1,0:T(8,128)(2,1)}, f32[7]{0:T(128)}) custom-call(f32[7,72,512]{2,1,0:T(8,128)S(1)} %get-tuple-element.35.refs_0_, s16[512,512]{1,0:T(8,128)(2,1)S(1)} %collective-permute-done.refs_1_, s16[440,512]{1,0:T(8,128)(2,1)S(1)} %collective-permute-done.1.refs_2_, s16[368,512]{1,0:T(8,128)(2,1)S(1)} %collective-permute-done.2.refs_3_, ...), custom_call_target="tpu_custom_call" | custom-call | tf_op jit(solution)/shard_map/finish/pallas_call | solution.py:400
Async XLA Ops:
  10.3 32.9 %collective-permute-start = (s16[512,512]{1,0:T(8,128)(2,1)S(1)}, s16[512,512]{1,0:T(8,128)(2,1)S(1)}, u32[]{:S(2)}, u32[]{:S(2)}) collective-permute-start(s16[512,512]{1,0:T(8,128)(2,1)S(1)} %get-tuple-element.36), channel_id=1, source_target_pairs={{0,1},{1,0},{2,3},{3,2},{4,5},{5,4},{6,7},{7,6},{8,9},{9,8},{10,11... | collective-permute-start | bytes 1572872 | tf_op jit(solution)/shard_map/ppermute | solution.py:420
  11.7 31.4 %collective-permute-start.1 = (s16[440,512]{1,0:T(8,128)(2,1)S(1)}, s16[440,512]{1,0:T(8,128)(2,1)S(1)}, u32[]{:S(2)}, u32[]{:S(2)}) collective-permute-start(s16[440,512]{1,0:T(8,128)(2,1)S(1)} %get-tuple-element.37), channel_id=1, source_target_pairs={{0,2},{1,3},{2,0},{3,1},{4,6},{5,7},{6,4},{7,5},{8,10},{9,11},{10,... | collective-permute-start | bytes 1351688 | tf_op jit(solution)/shard_map/ppermute | solution.py:420
  14.8 28.4 %collective-permute-start.2 = (s16[368,512]{1,0:T(8,128)(2,1)S(1)}, s16[368,512]{1,0:T(8,128)(2,1)S(1)}, u32[]{:S(2)}, u32[]{:S(2)}) collective-permute-start(s16[368,512]{1,0:T(8,128)(2,1)S(1)} %get-tuple-element.38), channel_id=1, source_target_pairs={{0,3},{1,2},{2,1},{3,0},{4,7},{5,6},{6,5},{7,4},{8,11},{9,10},{10,... | collective-permute-start | bytes 1130504 | tf_op jit(solution)/shard_map/ppermute | solution.py:420
  15.0 28.2 %collective-permute-start.4 = (s16[152,512]{1,0:T(8,128)(2,1)S(1)}, s16[152,512]{1,0:T(8,128)(2,1)S(1)}, u32[]{:S(2)}, u32[]{:S(2)}) collective-permute-start(s16[152,512]{1,0:T(8,128)(2,1)S(1)} %get-tuple-element.40), channel_id=1, source_target_pairs={{0,3},{1,2},{2,1},{3,0},{4,7},{5,6},{6,5},{7,4},{8,11},{9,10},{10,... | collective-permute-start | bytes 466952 | tf_op jit(solution)/shard_map/ppermute | solution.py:420
  18.0 25.1 %collective-permute-start.3 = (s16[80,512]{1,0:T(8,128)(2,1)S(1)}, s16[80,512]{1,0:T(8,128)(2,1)S(1)}, u32[]{:S(2)}, u32[]{:S(2)}) collective-permute-start(s16[80,512]{1,0:T(8,128)(2,1)S(1)} %get-tuple-element.39), channel_id=1, source_target_pairs={{0,2},{1,3},{2,0},{3,1},{4,6},{5,7},{6,4},{7,5},{8,10},{9,11},{10,... | collective-permute-start | bytes 245768 | tf_op jit(solution)/shard_map/ppermute | solution.py:420
